TPU v7x, 32 devices: a whole 2x2x4 slice. The times are simulated.
32 devices in a mesh: dp: 8 (over z, x), tensor: 4 (over y, core).
Axes of the slice: x: 2, y: 2, z: 4, core: 2. Of those that a mesh axis runs over, the one named last changes fastest.
Arguments:
- residual_in: float32 [16384, 768], P(('dp', 'tensor')), may hold values from -6 to 6
- out_grad: float32 [16384, 768], P(('dp', 'tensor')), may hold values from -6 to 6
- seq_lengths: int32 [8, 16], P('dp'), may hold values from 0 to 1024, as said below
- timesteps: int32 [8, 16], P('dp'), may hold values from 0 to 1023
- norm_gain: float32 [768], replicated, may hold values from 0.5 to 1.5
- norm_bias: float32 [768], replicated, may hold values from -3 to 3
- qkv_weight: float32 [3, 768, 768], P(None, 'dp', 'tensor'), may hold values from -0.21875 to 0.21875
- proj_weight: float32 [768, 768], P('tensor', 'dp'), may hold values from -0.875 to 0.875
- proj_bias: float32 [768], replicated, may hold values from -2 to 2
- up_weight: float32 [768, 3072], P('dp', 'tensor'), may hold values from -0.21875 to 0.21875
- up_bias: float32 [3072], replicated, may hold values from -3 to 3
- down_weight: float32 [3072, 768], P('tensor', 'dp'), may hold values from -0.109375 to 0.109375
- down_bias: float32 [768], replicated, may hold values from -2 to 2
- time_weight: float32 [128, 2304], replicated, may hold values from -0.5 to 0.5
- time_bias: float32 [2304], replicated, may hold values from -3 to 3
Outputs:
- residual_out: float32 [16384, 768], P(('dp', 'tensor'))
- input_grad: float32 [16384, 768], P(('dp', 'tensor'))
- norm_gain_grad: float32 [768], replicated
- norm_bias_grad: float32 [768], replicated
- qkv_weight_grad: float32 [3, 768, 768], P(None, 'dp', 'tensor')
- proj_weight_grad: float32 [768, 768], P('tensor', 'dp')
- proj_bias_grad: float32 [768], replicated
- up_weight_grad: float32 [768, 3072], P('dp', 'tensor')
- up_bias_grad: float32 [3072], replicated
- down_weight_grad: float32 [3072, 768], P('tensor', 'dp')
- down_bias_grad: float32 [768], replicated
- time_weight_grad: float32 [128, 2304], replicated
- time_bias_grad: float32 [2304], replicated
Inputs may be any that keep to these rules, and one draw needn't show every extreme that they name: `seq_lengths`: row g lists the lengths of the sequences packed in order into the 2048 rows of pack g: the nonzero lengths come first and lie between 128 and 1024, their sum is at most 2048, the rows after it are padding, and every row holds a length of exactly 1024.
All inputs are finite; a program needn't handle non-finite values.
Results may differ from a plain program's by a relative error of at most 0.015.
Values may be sent and summed in bfloat16 or wider, within the bound.
A program may use at most 128 MiB of HBM per device.

v0:
```python
import functools
import math

import jax
import jax.numpy as jnp
from jax import lax
from jax.experimental import pallas as pl
from jax.experimental.pallas import tpu as pltpu
from jax.sharding import PartitionSpec as P


HDIM = 64
HALF = HDIM // 2
BQ = 256
BK = 256
NEG = -1000000000.0
MESH = pl.DeviceIdType.MESH
BF = jnp.bfloat16
F32 = jnp.float32
VMEM_LIMIT = 60 * 1024 * 1024


highest = lax.Precision.HIGHEST


def dot(a, b, ca, cb, out=F32):
    return lax.dot_general(a, b, (((ca,), (cb,)), ((), ())), preferred_element_type=out)


def normalize(values):
    center = values - jnp.mean(values, axis=-1, keepdims=True)
    inverse = lax.rsqrt(jnp.mean(center * center, axis=-1, keepdims=True) + 1e-05)
    return (center * inverse, inverse)


def norm_back(grad_in, normed, inverse):
    return inverse * (
        grad_in
        - jnp.mean(grad_in, axis=-1, keepdims=True)
        - normed * jnp.mean(grad_in * normed, axis=-1, keepdims=True)
    )


def pack_info(lengths, row_total):
    row_index = jnp.arange(row_total, dtype=jnp.int32)
    seq_ends = jnp.cumsum(lengths)
    passed = row_index[:, None] >= seq_ends[None, :]
    segment = jnp.sum(passed.astype(jnp.int32), axis=1)
    starts = jnp.sum(jnp.where(passed, lengths[None, :], 0), axis=1)
    return (segment, row_index - starts)


def key_ranges(lengths, row_total):
    seq_ends = jnp.cumsum(lengths)
    first = jnp.arange(row_total // BQ, dtype=jnp.int32) * BQ
    last = first + (BQ - 1)
    start = jnp.sum(jnp.where(first[:, None] >= seq_ends[None, :], lengths[None, :], 0), axis=1)
    end = jnp.min(jnp.where(seq_ends[None, :] > last[:, None], seq_ends[None, :], row_total), axis=1)
    return (start // BK).astype(jnp.int32), ((end + BK - 1) // BK).astype(jnp.int32)


def time_embed(time_index, embed_width):
    half_width = embed_width // 2
    freqs = jnp.exp(-math.log(10000.0) * jnp.arange(half_width, dtype=jnp.float32) / half_width)
    angles = time_index.astype(jnp.float32)[:, None] * freqs[None, :]
    return jnp.concatenate([jnp.cos(angles), jnp.sin(angles)], axis=1)


def rope_tables(positions):
    inverse = jnp.exp(-math.log(10000.0) * jnp.arange(HALF, dtype=jnp.float32) * (2.0 / HDIM))
    angles = inverse[:, None] * positions.astype(jnp.float32)[None, :]
    return (jnp.cos(angles), jnp.sin(angles))


def project_kernel(heads, n_ref, w_ref, cos_ref, sin_ref, q_ref, k_ref, v_ref):
    width = heads * HDIM
    raw = dot(w_ref[...], n_ref[...], 1, 1)
    cos = cos_ref[...]
    sin = sin_ref[...]
    for part, out_ref, factor in ((0, q_ref, 1.0 / math.sqrt(HDIM)), (1, k_ref, 1.0)):
        for h in range(heads):
            base = part * width + h * HDIM
            a = raw[base : base + HALF]
            b = raw[base + HALF : base + HDIM]
            out_ref[h * HDIM : h * HDIM + HALF] = ((a * cos - b * sin) * factor).astype(BF)
            out_ref[h * HDIM + HALF : (h + 1) * HDIM] = ((b * cos + a * sin) * factor).astype(BF)
    v_ref[...] = raw[2 * width :].astype(BF)


def project(normed, weight_t, cos, sin, heads):
    rows, width_model = normed.shape
    width = heads * HDIM
    tile = 512
    out = jax.ShapeDtypeStruct((width, rows), BF)
    spec = pl.BlockSpec((width, tile), lambda i: (0, i))
    return pl.pallas_call(
        functools.partial(project_kernel, heads),
        name="project_qkv",
        grid=(rows // tile,),
        in_specs=[
            pl.BlockSpec((tile, width_model), lambda i: (i, 0)),
            pl.BlockSpec((3 * width, width_model), lambda i: (0, 0)),
            pl.BlockSpec((HALF, tile), lambda i: (0, i)),
            pl.BlockSpec((HALF, tile), lambda i: (0, i)),
        ],
        out_specs=[spec, spec, spec],
        out_shape=[out, out, out],
        cost_estimate=pl.CostEstimate(
            flops=2 * rows * width_model * 3 * width, bytes_accessed=8 << 20, transcendentals=0
        ),
    )(normed, weight_t, cos, sin)


def wide(column, lanes):
    return jnp.concatenate([column] * (lanes // 128), axis=1)


def attend_kernel(
    heads, lo_ref, hi_ref, q_ref, k_ref, v_ref, srow_ref, scol_ref, o_ref, lse_ref, kt_ref, sc_ref
):
    i = pl.program_id(0)

    @pl.when(i == 0)
    def _():
        for h in range(heads):
            kt_ref[h] = k_ref[h * HDIM : (h + 1) * HDIM, :].T
        sc_ref[...] = jnp.broadcast_to(scol_ref[...], sc_ref.shape)

    srow = srow_ref[...]

    def step(j, carry):
        base = pl.multiple_of(j * BK, BK)
        allowed = wide(sc_ref[pl.ds(base, BK), :], BQ) == srow
        out = []
        for h in range(heads):
            m, l, acc = carry[h]
            s = dot(kt_ref[h, pl.ds(base, BK), :], q_ref[h * HDIM : (h + 1) * HDIM, :], 1, 0)
            s = jnp.where(allowed, s, NEG)
            m_new = jnp.maximum(m, jnp.max(s, axis=0, keepdims=True))
            fade = jnp.exp(m - m_new)
            p = jnp.exp(s - m_new)
            l = fade * l + jnp.sum(p, axis=0, keepdims=True)
            acc = fade * acc + dot(
                v_ref[h * HDIM : (h + 1) * HDIM, pl.ds(base, BK)], p.astype(BF), 1, 0
            )
            out.append((m_new, l, acc))
        return tuple(out)

    empty = (
        jnp.full((1, BQ), -3.0e38, F32),
        jnp.zeros((1, BQ), F32),
        jnp.zeros((HDIM, BQ), F32),
    )
    done = lax.fori_loop(lo_ref[i], hi_ref[i], step, (empty,) * heads)
    for h in range(heads):
        m, l, acc = done[h]
        o_ref[h * HDIM : (h + 1) * HDIM, :] = (acc / l).astype(BF)
        lse_ref[h : h + 1, :] = m + jnp.log(l)


def attend(q, k, v, seg_row, seg_col, lo, hi):
    width, rows = q.shape
    heads = width // HDIM
    whole = lambda i, *_: (0, 0)
    block = lambda i, *_: (0, i)
    return pl.pallas_call(
        functools.partial(attend_kernel, heads),
        name="attend",
        grid_spec=pltpu.PrefetchScalarGridSpec(
            num_scalar_prefetch=2,
            grid=(rows // BQ,),
            in_specs=[
                pl.BlockSpec((width, BQ), block),
                pl.BlockSpec((width, rows), whole),
                pl.BlockSpec((width, rows), whole),
                pl.BlockSpec((1, BQ), block),
                pl.BlockSpec((rows, 1), whole),
            ],
            out_specs=[
                pl.BlockSpec((width, BQ), block),
                pl.BlockSpec((heads, BQ), block),
            ],
            scratch_shapes=[
                pltpu.VMEM((heads, rows, HDIM), BF),
                pltpu.VMEM((rows, 128), jnp.int32),
            ],
        ),
        out_shape=[
            jax.ShapeDtypeStruct((width, rows), BF),
            jax.ShapeDtypeStruct((heads, rows), F32),
        ],
        compiler_params=pltpu.CompilerParams(vmem_limit_bytes=VMEM_LIMIT),
        cost_estimate=pl.CostEstimate(
            flops=rows * rows * heads * HDIM * 8, bytes_accessed=8 << 20, transcendentals=rows * rows
        ),
    )(lo, hi, q, k, v, seg_row, seg_col)


def attend_back_kernel(
    heads,
    lo_ref,
    hi_ref,
    q_ref,
    k_ref,
    v_ref,
    do_ref,
    o_ref,
    lse_ref,
    srow_ref,
    scol_ref,
    cos_ref,
    sin_ref,
    g_ref,
    kt_ref,
    vt_ref,
    sc_ref,
    dk_ref,
    dv_ref,
):
    i = pl.program_id(0)
    width = heads * HDIM

    @pl.when(i == 0)
    def _():
        for h in range(heads):
            kt_ref[h] = k_ref[h * HDIM : (h + 1) * HDIM, :].T
            vt_ref[h] = v_ref[h * HDIM : (h + 1) * HDIM, :].T
        sc_ref[...] = jnp.broadcast_to(scol_ref[...], sc_ref.shape)
        dk_ref[...] = jnp.zeros_like(dk_ref)
        dv_ref[...] = jnp.zeros_like(dv_ref)

    srow = srow_ref[...]
    inner = []
    for h in range(heads):
        part = slice(h * HDIM, (h + 1) * HDIM)
        inner.append(
            jnp.sum(do_ref[part, :].astype(F32) * o_ref[part, :].astype(F32), axis=0, keepdims=True)
        )

    def step(j, carry):
        base = pl.multiple_of(j * BK, BK)
        keys = pl.ds(base, BK)
        allowed = wide(sc_ref[keys, :], BQ) == srow
        out = []
        for h in range(heads):
            part = slice(h * HDIM, (h + 1) * HDIM)
            q = q_ref[part, :]
            grad = do_ref[part, :]
            s = dot(kt_ref[h, keys, :], q, 1, 0)
            s = jnp.where(allowed, s, NEG)
            p = jnp.exp(s - lse_ref[h : h + 1, :])
            dp = dot(vt_ref[h, keys, :], grad, 1, 0)
            ds = (p * (dp - inner[h])).astype(BF)
            out.append(carry[h] + dot(k_ref[part, keys], ds, 1, 0))
            dk_ref[part, keys] += dot(q, ds, 1, 1)
            dv_ref[part, keys] += dot(grad, p.astype(BF), 1, 1)
        return tuple(out)

    done = lax.fori_loop(
        lo_ref[i], hi_ref[i], step, (jnp.zeros((HDIM, BQ), F32),) * heads
    )
    here = pl.ds(pl.multiple_of(i * BQ, BQ), BQ)
    cos = cos_ref[:, here]
    sin = sin_ref[:, here]
    factor = 1.0 / math.sqrt(HDIM)
    for h in range(heads):
        a = done[h][:HALF] * factor
        b = done[h][HALF:] * factor
        g_ref[h * HDIM : h * HDIM + HALF, here] = (a * cos + b * sin).astype(BF)
        g_ref[h * HDIM + HALF : (h + 1) * HDIM, here] = (b * cos - a * sin).astype(BF)

    @pl.when(i == pl.num_programs(0) - 1)
    def _():
        cos_all = cos_ref[...]
        sin_all = sin_ref[...]
        for h in range(heads):
            a = dk_ref[h * HDIM : h * HDIM + HALF, :]
            b = dk_ref[h * HDIM + HALF : (h + 1) * HDIM, :]
            base = width + h * HDIM
            g_ref[base : base + HALF, :] = (a * cos_all + b * sin_all).astype(BF)
            g_ref[base + HALF : base + HDIM, :] = (b * cos_all - a * sin_all).astype(BF)
        g_ref[2 * width :, :] = dv_ref[...].astype(BF)


def attend_back(q, k, v, do, o, lse, seg_row, seg_col, cos, sin, lo, hi):
    width, rows = q.shape
    heads = width // HDIM
    whole = lambda i, *_: (0, 0)
    block = lambda i, *_: (0, i)
    return pl.pallas_call(
        functools.partial(attend_back_kernel, heads),
        name="attend_back",
        grid_spec=pltpu.PrefetchScalarGridSpec(
            num_scalar_prefetch=2,
            grid=(rows // BQ,),
            in_specs=[
                pl.BlockSpec((width, BQ), block),
                pl.BlockSpec((width, rows), whole),
                pl.BlockSpec((width, rows), whole),
                pl.BlockSpec((width, BQ), block),
                pl.BlockSpec((width, BQ), block),
                pl.BlockSpec((heads, BQ), block),
                pl.BlockSpec((1, BQ), block),
                pl.BlockSpec((rows, 1), whole),
                pl.BlockSpec((HALF, rows), whole),
                pl.BlockSpec((HALF, rows), whole),
            ],
            out_specs=pl.BlockSpec((3 * width, rows), whole),
            scratch_shapes=[
                pltpu.VMEM((heads, rows, HDIM), BF),
                pltpu.VMEM((heads, rows, HDIM), BF),
                pltpu.VMEM((rows, 128), jnp.int32),
                pltpu.VMEM((width, rows), F32),
                pltpu.VMEM((width, rows), F32),
            ],
        ),
        out_shape=jax.ShapeDtypeStruct((3 * width, rows), BF),
        compiler_params=pltpu.CompilerParams(vmem_limit_bytes=VMEM_LIMIT),
        cost_estimate=pl.CostEstimate(
            flops=rows * rows * heads * HDIM * 20, bytes_accessed=8 << 20, transcendentals=rows * rows
        ),
    )(lo, hi, q, k, v, do, o, lse, seg_row, seg_col, cos, sin)


class Links:
    def __init__(self, send_sem, recv_sem, n_z):
        dp = lax.axis_index("dp")
        t = lax.axis_index("tensor")
        self.n_z, self.dp, self.t = n_z, dp, t
        self.z, self.x = dp // 2, dp % 2
        self.y, self.c = t // 2, t % 2
        self.core_rank = 2 * self.y + (1 - self.c)
        self.y_rank = 2 * (1 - self.y) + self.c
        self.core = {"tensor": self.core_rank}
        self.across = {"tensor": self.y_rank}
        self.beside = {"dp": 2 * self.z + (1 - self.x)}
        self.send_sem, self.recv_sem = send_sem, recv_sem
        self.slot = 0

    def along(self, step):
        return {"dp": 2 * ((self.z + step) % self.n_z) + self.x}

    def slots(self, count):
        first = self.slot
        self.slot += count
        return first

    def copy(self, src, dst, peer, slot):
        return pltpu.make_async_remote_copy(
            src_ref=src,
            dst_ref=dst,
            send_sem=self.send_sem.at[slot],
            recv_sem=self.recv_sem.at[slot],
            device_id=peer,
            device_id_type=MESH,
        )

    def send(self, src, dst, peer):
        copy = self.copy(src, dst, peer, self.slots(1))
        copy.start()
        return copy


def greet(peers):
    barrier = pltpu.get_barrier_semaphore()
    for peer in peers:
        pl.semaphore_signal(barrier, inc=1, device_id=peer, device_id_type=MESH)
    pl.semaphore_wait(barrier, len(peers))


def opening_kernel(n_z, count, *refs):
    n_ref, w_refs = refs[0], refs[1 : 1 + count]
    n_out, w_outs = refs[1 + count], refs[2 + count : 2 + 2 * count]
    local_sem, send_sem, recv_sem = refs[2 + 2 * count :]
    links = Links(send_sem, recv_sem, n_z)
    greet([links.core, links.across, links.beside] + [links.along(k) for k in range(1, n_z)])
    rows = n_ref.shape[0]

    def n_at(rank):
        return n_out.at[pl.ds(pl.multiple_of(rank * rows, rows), rows)]

    def w_at(n, rank):
        return w_outs[n].at[0, rank] if n in (1, 2) else w_outs[n].at[rank]

    crossed = []

    def cross(rank):
        crossed.append(links.send(w_outs[2].at[0, rank], w_outs[2].at[1, rank], links.across))

    n_y = links.send(n_ref, n_at(links.t), links.across)
    near, far = [], []
    for n in range(count):
        near.append([links.send(w_refs[n], w_at(n, links.dp), links.along(k)) for k in range(1, n_z)])
        far.append([links.send(w_refs[n], w_at(n, links.dp), links.beside)])
    n_core = links.send(n_ref, n_at(links.t), links.core)
    local = [pltpu.make_async_copy(n_ref, n_at(links.t), local_sem.at[0])]
    for n in range(count):
        local.append(pltpu.make_async_copy(w_refs[n], w_at(n, links.dp), local_sem.at[1 + n]))
    for copy in local:
        copy.start()
    others = []
    for n in range(count):
        for k in range(1, n_z):
            near[n][k - 1].wait_recv()
            rank = 2 * ((links.z + n_z - k) % n_z) + links.x
            far[n].append(links.send(w_at(n, rank), w_at(n, rank), links.beside))
            if n == 2:
                cross(rank)
        if n == 2:
            local[1 + n].wait()
            cross(links.dp)
        if n == 1:
            n_y.wait_recv()
            n_relay = links.send(n_at(links.y_rank), n_at(links.y_rank), links.core)
            for copy in far[n]:
                copy.wait_recv()
            local[1 + n].wait()
            others.append(links.send(w_outs[n].at[0], w_outs[n].at[2], links.across))
            others.append(links.send(w_outs[n].at[0], w_outs[n].at[1], links.core))
    for k in range(n_z):
        far[2][k].wait_recv()
        cross(2 * ((links.z + n_z - k) % n_z) + 1 - links.x)
    others[0].wait_recv()
    others.append(links.send(w_outs[1].at[2], w_outs[1].at[3], links.core))
    n_core.wait_recv()
    n_relay.wait_recv()
    others[1].wait_recv()
    others[2].wait_recv()
    for n in range(count):
        if n not in (1, 2):
            for copy in far[n]:
                copy.wait_recv()
            local[1 + n].wait()
        for copy in near[n] + far[n]:
            copy.wait_send()
    for copy in crossed:
        copy.wait_recv()
    for copy in [n_y, n_core, n_relay] + others + crossed:
        copy.wait_send()
    local[0].wait()


def opening(normed, weights, n_dp, n_tensor):
    rows, width = normed.shape
    n_z = n_dp // 2
    count = len(weights)
    slots = count * (2 * n_z - 1) + 6 + n_dp
    shapes = [(n_dp,) + w.shape for w in weights]
    shapes[1] = (n_tensor,) + shapes[1]
    shapes[2] = (2,) + shapes[2]
    return pl.pallas_call(
        functools.partial(opening_kernel, n_z, count),
        name="opening",
        in_specs=[pl.BlockSpec(memory_space=pltpu.VMEM)] * (1 + count),
        out_specs=[pl.BlockSpec(memory_space=pl.ANY)] * (1 + count),
        out_shape=[jax.ShapeDtypeStruct((n_tensor * rows, width), BF)]
        + [jax.ShapeDtypeStruct(shape, BF) for shape in shapes],
        scratch_shapes=[
            pltpu.SemaphoreType.DMA((1 + count,)),
            pltpu.SemaphoreType.DMA((slots,)),
            pltpu.SemaphoreType.DMA((slots,)),
        ],
        compiler_params=pltpu.CompilerParams(collective_id=0, has_side_effects=True),
        cost_estimate=pl.CostEstimate(flops=0, bytes_accessed=64 << 20, transcendentals=0),
    )(normed, *weights)


def closing_kernel(n_z, count, *refs):
    part_refs = refs[:4]
    w_refs = refs[4 : 4 + count]
    x_ref, h_ref, gain_ref, sums_ref = refs[4 + count : 8 + count]
    outs = refs[8 + count : 11 + 2 * count]
    in_grad_ref, tail_ref, all_ref, g_refs = outs[0], outs[1], outs[2], outs[3:]
    scratch = refs[11 + 2 * count :]
    core_buf, y_send, y_recv, vec, all_vec, sums_buf = scratch[:6]
    x_recv = scratch[6 : 6 + count]
    z_send = scratch[6 + count : 6 + 2 * count]
    z_recv = scratch[6 + 2 * count : 6 + 3 * count]
    send_sem, recv_sem = scratch[6 + 3 * count :]
    links = Links(send_sem, recv_sem, n_z)
    n_dp = 2 * n_z
    dp_peers = [{"dp": (links.dp + k) % n_dp} for k in range(1, n_dp)]
    diagonal = {"tensor": 3 - links.t}
    greet([links.core, links.across, diagonal] + dp_peers)

    c1 = links.send(part_refs[1], core_buf.at[0], links.core)
    c3 = links.send(part_refs[3], core_buf.at[1], links.core)
    quarter = sums_ref.shape[1] // 4

    def lanes(rank):
        return pl.ds(pl.multiple_of(rank * quarter, 128), quarter)

    ranks = (links.core_rank, links.y_rank, 3 - links.t)
    tensor_peers = (links.core, links.across, diagonal)
    sums_tensor = [
        links.send(sums_ref.at[:, lanes(rank)], sums_buf.at[links.t], peer)
        for rank, peer in zip(ranks, tensor_peers)
    ]
    sums_buf[links.t] = sums_ref[:, lanes(links.t)]
    x_slots = [links.slots(n_z) for _ in range(count)]
    z_slots = [links.slots(n_z) for _ in range(count)]

    def x_copy(n, s):
        target = (links.z + s) % n_z
        src = w_refs[n].at[target, 1 - links.x]
        return links.copy(src, x_recv[n].at[s], links.beside, x_slots[n] + s)

    def z_copy(n, s):
        peer = {"dp": 2 * ((links.z + s) % n_z) + links.x}
        return links.copy(z_send[n].at[s], z_recv[n].at[s], peer, z_slots[n] + s)

    def x_sum(n, s):
        x_copy(n, s).wait_recv()
        own = w_refs[n][(links.z + s) % n_z, links.x]
        return own.astype(F32) + x_recv[n][s].astype(F32)

    for n in range(count):
        for s in list(range(1, n_z)) + [0]:
            x_copy(n, s).start()

    c1.wait_recv()
    c3.wait_recv()
    y_send[...] = (part_refs[2][...].astype(F32) + core_buf[1].astype(F32)).astype(BF)
    for copy in sums_tensor:
        copy.wait_recv()
    own_lanes = lanes(links.t)
    all_ref[links.dp, :, own_lanes] = sums_buf[0] + sums_buf[1] + sums_buf[2] + sums_buf[3]
    late = None
    y_copy = links.copy(y_send, y_recv, links.across, links.slots(1))
    started = False
    for n in range(count):
        for s in range(1, n_z):
            z_send[n][s] = x_sum(n, s).astype(BF)
            if not started:
                y_copy.start()
                started = True
                here = all_ref.at[links.dp, :, own_lanes]
                sums_dp = [links.send(here, here, peer) for peer in dp_peers]
            if late is not None:
                z_copy(*late).start()
            late = (n, s)
        g_refs[n][...] = x_sum(n, 0)
    z_copy(*late).start()

    for copy in sums_dp:
        copy.wait_recv()
    here = all_ref.at[:, :, own_lanes]
    there = all_ref.at[:, :, lanes(links.y_rank)]
    sums_last = [links.send(here, here, links.across), links.send(here, here, links.core)]
    y_copy.wait_recv()
    grad = part_refs[0][...].astype(F32) + core_buf[0].astype(F32) + y_recv[...].astype(F32)
    normed, inverse = normalize(x_ref[...])
    own_vec = jnp.concatenate(
        [jnp.sum(grad * normed, axis=0, keepdims=True), jnp.sum(grad, axis=0, keepdims=True)], axis=1
    )
    vec[links.t] = own_vec
    in_grad_ref[...] = h_ref[...] + norm_back(grad * gain_ref[...], normed, inverse)
    tensor_sends = [
        links.send(vec.at[links.t], vec.at[links.t], peer)
        for peer in (links.core, links.across, diagonal)
    ]
    sums_last[0].wait_recv()
    sums_last.append(links.send(there, there, links.core))
    for copy in tensor_sends:
        copy.wait()
    total = vec[0] + vec[1] + vec[2] + vec[3]
    all_vec[links.dp] = total
    for n in range(count):
        for s in range(1, n_z):
            z_copy(n, s).wait_recv()
            g_refs[n][...] += z_recv[n][s].astype(F32)
    dp_sends = [links.send(all_vec.at[links.dp], all_vec.at[links.dp], peer) for peer in dp_peers]
    for copy in dp_sends:
        copy.wait_recv()
    total = all_vec[0]
    for r in range(1, n_dp):
        total = total + all_vec[r]
    tail_ref[...] = total
    sums_last[1].wait_recv()
    sums_last[2].wait_recv()
    for copy in [c1, c3, y_copy] + dp_sends + sums_tensor + sums_dp + sums_last:
        copy.wait_send()
    for n in range(count):
        for s in range(n_z):
            x_copy(n, s).wait_send()
            if s > 0:
                z_copy(n, s).wait_send()


def closing(parts, weights, residual_in, hidden_grad, gain, sums, n_dp):
    rows, width = residual_in.shape
    n_z = n_dp // 2
    count = len(weights)
    blocks = [w.reshape(n_z, 2, w.shape[0] // n_dp, w.shape[1]) for w in weights]
    shards = [b.shape[2:] for b in blocks]
    slots = 2 + 2 * count * n_z + 1 + 3 + (n_dp - 1) + 3 + (n_dp - 1) + 3
    vmem = pl.BlockSpec(memory_space=pltpu.VMEM)
    out = pl.pallas_call(
        functools.partial(closing_kernel, n_z, count),
        name="closing",
        in_specs=[vmem] * (8 + count),
        out_specs=[vmem] * (3 + count),
        out_shape=[
            jax.ShapeDtypeStruct((rows, width), F32),
            jax.ShapeDtypeStruct((1, 2 * width), F32),
            jax.ShapeDtypeStruct((n_dp,) + sums.shape, F32),
        ]
        + [jax.ShapeDtypeStruct(shape, F32) for shape in shards],
        scratch_shapes=[
            pltpu.VMEM((2, rows, width), BF),
            pltpu.VMEM((rows, width), BF),
            pltpu.VMEM((rows, width), BF),
            pltpu.VMEM((4, 1, 2 * width), F32),
            pltpu.VMEM((n_dp, 1, 2 * width), F32),
            pltpu.VMEM((4, sums.shape[0], sums.shape[1] // 4), F32),
        ]
        + [pltpu.VMEM((n_z,) + shape, BF) for _ in range(3) for shape in shards]
        + [pltpu.SemaphoreType.DMA((slots,)), pltpu.SemaphoreType.DMA((slots,))],
        compiler_params=pltpu.CompilerParams(
            collective_id=1, has_side_effects=True, vmem_limit_bytes=VMEM_LIMIT
        ),
        cost_estimate=pl.CostEstimate(flops=0, bytes_accessed=64 << 20, transcendentals=0),
    )(*parts, *blocks, residual_in, hidden_grad, gain[None, :], sums)
    return out[0], out[1].reshape(2, width), out[2], out[3:]


ROWS = 128
STRIP = 256


def middle_kernel(slots, *refs):
    (
        mixed_ref,
        proj_ref,
        up_hbm,
        down_hbm,
        down_far_hbm,
        x_ref,
        grad_ref,
        mod_ref,
        sel_ref,
        embed_ref,
        proj_bias_ref,
        up_bias_ref,
        down_bias_ref,
    ) = refs[:13]
    out_ref, h_grad_ref, mixed_grad_ref, sums_ref, up_near, down_near, proj_near, far, proj_far = refs[
        13:22
    ]
    (
        mix_buf,
        mix_t,
        up_buf,
        down_buf,
        hid_s,
        m_s,
        flip_s,
        dz_s,
        dz_t,
        act_s,
        du_s,
        z_acc,
        m_acc,
        up_send,
        down_send,
        up_recv,
        down_recv,
        low_s,
        back_s,
        proj_send,
        proj_recv,
        local_sem,
        send_sem,
        recv_sem,
    ) = refs[22:]
    links = Links(send_sem, recv_sem, slots)
    rows, width = x_ref.shape
    peers = [None, links.core, links.across, {"tensor": 3 - links.t}]
    ranks = [links.t, links.core_rank, links.y_rank, 3 - links.t]
    greet(peers[1:])

    def lanes(rank):
        return pl.ds(pl.multiple_of(rank * rows, rows), rows)

    mix_copies = [
        links.send(mixed_ref.at[:, lanes(ranks[d])], mix_buf.at[d], peers[d]) for d in (3, 2, 1)
    ]
    w_copies = [
        links.send(up_hbm.at[0], up_buf.at[1], links.core),
        links.send(down_hbm, down_buf.at[1], links.core),
        links.send(up_hbm.at[1], up_buf.at[3], links.core),
        links.send(down_far_hbm, down_buf.at[3], links.core),
    ]
    local = [
        pltpu.make_async_copy(up_hbm.at[0], up_buf.at[0], local_sem.at[0]),
        pltpu.make_async_copy(down_hbm, down_buf.at[0], local_sem.at[1]),
        pltpu.make_async_copy(up_hbm.at[1], up_buf.at[2], local_sem.at[2]),
        pltpu.make_async_copy(down_far_hbm, down_buf.at[2], local_sem.at[3]),
    ]
    for copy in local:
        copy.start()

    def tiles(body, carry=0):
        return lax.fori_loop(0, rows // ROWS, body, carry)

    def tile(i):
        return pl.ds(pl.multiple_of(i * ROWS, ROWS), ROWS)

    def gate_step(i, total):
        here = tile(i)
        dz = grad_ref[here, :] * mod_ref[here, 2 * width :]
        dz_s[here, :] = dz.astype(BF)
        return total + jnp.sum(dz, axis=0, keepdims=True)

    down_bias_sum = tiles(gate_step, jnp.zeros((1, width), F32))
    dz_t[...] = dz_s[...].T
    sums_ref[...] = jnp.zeros_like(sums_ref)
    mix_t[0] = mixed_ref[:, lanes(links.t)].T
    for d, copy in zip((3, 2, 1), mix_copies):
        copy.wait_recv()
        mix_t[d] = mix_buf[d].T

    def hidden_step(i, carry):
        here = tile(i)
        hidden = x_ref[here, :] + proj_bias_ref[...]
        for d in range(4):
            hidden = hidden + dot(mix_t[d, here, :], proj_ref[d], 1, 1)
        hid_s[here, :] = hidden
        normed, _ = normalize(hidden)
        scale = mod_ref[here, :width]
        shift = mod_ref[here, width : 2 * width]
        m_s[here, :] = (normed * (1.0 + scale) + shift).astype(BF)
        return carry

    tiles(hidden_step)
    flip_s[...] = m_s[...].T
    z_acc[...] = jnp.zeros_like(z_acc)
    m_acc[...] = jnp.zeros_like(m_acc)
    root = math.sqrt(2.0 / math.pi)

    def feed(d):
        up = up_buf.at[d]
        down = down_buf.at[d]

        def step(i, total):
            here = pl.ds(pl.multiple_of(i * STRIP, STRIP), STRIP)
            u = dot(m_s[here, :], up[...], 1, 0) + up_bias_ref[d]
            square = u * u
            bend = jnp.tanh(root * u * (1.0 + 0.044715 * square))
            half = 0.5 * (1.0 + bend)
            act = (u * half).astype(BF)
            act_s[here, :] = act
            slope = half + 0.5 * u * (1.0 - bend * bend) * (root * (1.0 + 3.0 * 0.044715 * square))
            du = dot(dz_s[here, :], down[...], 1, 0) * slope
            low = du.astype(BF)
            du_s[here, :] = low
            z_acc[here, :] += dot(act, down[...], 1, 1)
            m_acc[here, :] += dot(low, up[...], 1, 1)
            return total + jnp.sum(low.astype(F32), axis=0, keepdims=True)

        total = lax.fori_loop(0, rows // STRIP, step, jnp.zeros((1, width), F32))
        y, c = (d // 2), (d % 2)
        rank = 2 * (y + links.y - 2 * y * links.y) + (c + links.c - 2 * c * links.c)
        sums_ref[pl.ds(17 + rank, 1), :width] = total

    def grads(store):
        def step(j, carry):
            here = pl.ds(pl.multiple_of(j * STRIP, STRIP), STRIP)
            store(here, dot(flip_s[here, :], du_s[...], 1, 0), dot(dz_t[here, :], act_s[...], 1, 0))
            return carry

        lax.fori_loop(0, width // STRIP, step, 0)

    for copy in w_copies:
        copy.wait_recv()

    def outward(e, carry):
        feed(2 * e + 1)

        def store(here, up_part, down_part):
            up_send[e, here, :] = up_part.astype(BF)
            down_send[e, here, :] = down_part.astype(BF)

        grads(store)
        return carry

    lax.fori_loop(0, 2, outward, 0)
    first = links.slots(2)
    second = links.slots(2)

    def up_copy(e):
        return links.copy(up_send.at[e], up_recv.at[e], links.core, first + e)

    def down_copy(e):
        return links.copy(down_send.at[e], down_recv.at[e], links.core, second + e)

    for e in range(2):
        up_copy(e).start()
        down_copy(e).start()
    for copy in local:
        copy.wait()

    for e, up_out, down_out in ((1, far.at[0], far.at[1]), (0, up_near, down_near)):
        feed(2 * e)
        up_copy(e).wait_recv()
        down_copy(e).wait_recv()

        def store(here, up_part, down_part):
            up_out[here, :] = (up_part + up_recv[e, here, :].astype(F32)).astype(BF)
            down_out[here, :] = (down_part + down_recv[e, here, :].astype(F32)).astype(BF)

        grads(store)

    def back_step(i, total):
        here = tile(i)
        hidden = hid_s[here, :]
        normed, inverse = normalize(hidden)
        scale = mod_ref[here, :width]
        gate = mod_ref[here, 2 * width :]
        grad = grad_ref[here, :]
        branch = z_acc[here, :] + down_bias_ref[...]
        shift_grad = m_acc[here, :]
        out_ref[here, :] = hidden + gate * branch
        h_grad = grad + norm_back(shift_grad * (1.0 + scale), normed, inverse)
        h_grad_ref[here, :] = h_grad
        low_s[here, :] = h_grad.astype(BF)
        sel = sel_ref[:, here]
        for part, value in ((0, shift_grad * normed), (1, shift_grad), (2, grad * branch)):
            sums_ref[:, part * width : (part + 1) * width] += lax.dot_general(
                sel, value, (((1,), (0,)), ((), ())), precision=highest, preferred_element_type=F32
            )
        return total + jnp.sum(h_grad, axis=0, keepdims=True)

    proj_bias_sum = tiles(back_step, jnp.zeros((1, width), F32))
    back_copies = []
    for d in (3, 2, 1, 0):
        part = dot(low_s[...], proj_ref[d], 1, 0).astype(BF).T
        if d == 0:
            mixed_grad_ref[:, lanes(links.t)] = part
        else:
            back_s[d] = part
        if d < 3:
            back_copies.append(
                links.send(back_s.at[d + 1], mixed_grad_ref.at[:, lanes(links.t)], peers[d + 1])
            )
    sums_ref[16:17, :width] = proj_bias_sum
    sums_ref[16:17, width : 2 * width] = down_bias_sum
    embed_at = 3 * width
    sums_ref[: embed_ref.shape[0], embed_at : embed_at + embed_ref.shape[1]] = embed_ref[...]
    flip_s[...] = low_s[...].T
    for d in (1, 3):
        proj_send[d // 2] = dot(flip_s[...], mix_t[d], 1, 0).astype(BF)
    own_part = dot(flip_s[...], mix_t[0], 1, 0)
    proj_copies = [links.send(proj_send.at[e], proj_recv.at[e], links.core) for e in range(2)]
    far_part = dot(flip_s[...], mix_t[2], 1, 0)
    for e, part, out in ((0, own_part, proj_near), (1, far_part, proj_far)):
        proj_copies[e].wait_recv()
        out[...] = (part + proj_recv[e].astype(F32)).astype(BF)
    for copy in back_copies:
        copy.wait_recv()
    for copy in mix_copies + w_copies + back_copies + proj_copies:
        copy.wait_send()
    for e in range(2):
        up_copy(e).wait_send()
        down_copy(e).wait_send()


def middle(mixed, proj, up, down, down_far, x, grad, mod, sel, embed, proj_bias, up_bias, down_bias):
    rows, width = x.shape
    head_width, total_rows = mixed.shape
    units = down.shape[1]
    vmem = pl.BlockSpec(memory_space=pltpu.VMEM)
    hbm = pl.BlockSpec(memory_space=pl.ANY)
    sums = (sel.shape[0], -(-(3 * width + embed.shape[1]) // 512) * 512)
    slots = 3 + 4 + 4 + 3 + 2
    square = (2, width, units)
    return pl.pallas_call(
        functools.partial(middle_kernel, 1),
        name="middle",
        in_specs=[vmem, vmem, hbm, hbm, hbm] + [vmem] * 8,
        out_specs=[vmem] * 9,
        out_shape=[
            jax.ShapeDtypeStruct((rows, width), F32),
            jax.ShapeDtypeStruct((rows, width), F32),
            jax.ShapeDtypeStruct((head_width, total_rows), BF),
            jax.ShapeDtypeStruct(sums, F32),
            jax.ShapeDtypeStruct(square[1:], BF),
            jax.ShapeDtypeStruct(square[1:], BF),
            jax.ShapeDtypeStruct((width, head_width), BF),
            jax.ShapeDtypeStruct(square, BF),
            jax.ShapeDtypeStruct((width, head_width), BF),
        ],
        scratch_shapes=[
            pltpu.VMEM((4, head_width, rows), BF),
            pltpu.VMEM((4, rows, head_width), BF),
            pltpu.VMEM((4, width, units), BF),
            pltpu.VMEM((4, width, units), BF),
            pltpu.VMEM((rows, width), F32),
            pltpu.VMEM((rows, width), BF),
            pltpu.VMEM((width, rows), BF),
            pltpu.VMEM((rows, width), BF),
            pltpu.VMEM((width, rows), BF),
            pltpu.VMEM((rows, units), BF),
            pltpu.VMEM((rows, units), BF),
            pltpu.VMEM((rows, width), F32),
            pltpu.VMEM((rows, width), F32),
            pltpu.VMEM(square, BF),
            pltpu.VMEM(square, BF),
            pltpu.VMEM(square, BF),
            pltpu.VMEM(square, BF),
            pltpu.VMEM((rows, width), BF),
            pltpu.VMEM((4, head_width, rows), BF),
            pltpu.VMEM((2, width, head_width), BF),
            pltpu.VMEM((2, width, head_width), BF),
            pltpu.SemaphoreType.DMA((4,)),
            pltpu.SemaphoreType.DMA((slots,)),
            pltpu.SemaphoreType.DMA((slots,)),
        ],
        compiler_params=pltpu.CompilerParams(
            collective_id=2, has_side_effects=True, vmem_limit_bytes=63 * 1024 * 1024
        ),
        cost_estimate=pl.CostEstimate(
            flops=12 * rows * width * units * 4, bytes_accessed=64 << 20, transcendentals=0
        ),
    )(mixed, proj, up, down, down_far, x, grad, mod, sel, embed, proj_bias, up_bias, down_bias)


def to_tensor_peer(value, distance):
    size = lax.axis_size("tensor")
    return lax.ppermute(value, "tensor", [(r, r ^ distance) for r in range(size)])


def shards(
    residual_in,
    out_grad,
    seq_lengths,
    timesteps,
    norm_gain,
    norm_bias,
    qkv_weight,
    proj_weight,
    proj_bias,
    up_weight,
    up_bias,
    down_weight,
    down_bias,
    time_weight,
    time_bias,
):
    row_count, width_model = residual_in.shape
    n_dp = lax.axis_size("dp")
    n_tensor = lax.axis_size("tensor")
    tensor_rank = lax.axis_index("tensor")
    total_rows = row_count * n_tensor
    slot_count = seq_lengths.shape[1]
    head_width = qkv_weight.shape[2]
    heads = head_width // HDIM
    units = up_weight.shape[1]
    ranks = [tensor_rank ^ d for d in range(n_tensor)]

    normed_in, _ = normalize(residual_in)
    normed_low = (normed_in * norm_gain + norm_bias).astype(BF)
    qkv_shard = jnp.transpose(qkv_weight, (1, 0, 2)).reshape(qkv_weight.shape[1], -1).astype(BF)
    normed_full, qkv_full, proj_all, up_own, down_own = opening(
        normed_low,
        (
            qkv_shard,
            proj_weight.T.astype(BF),
            up_weight.astype(BF),
            down_weight.T.astype(BF),
        ),
        n_dp,
        n_tensor,
    )
    qkv_full = qkv_full.reshape(width_model, -1)
    proj_all = proj_all.reshape(n_tensor, width_model, -1)
    up_both = up_own.reshape(2, width_model, -1)
    down_own = down_own.reshape(width_model, -1)
    down_far = to_tensor_peer(down_own, 2)

    segment, positions = pack_info(seq_lengths[0], total_rows)
    lo, hi = key_ranges(seq_lengths[0], total_rows)
    own_segment = lax.dynamic_slice_in_dim(segment, tensor_rank * row_count, row_count)
    slots = jnp.arange(slot_count, dtype=jnp.int32)
    onehot = (own_segment[:, None] == slots[None, :]).astype(F32)
    embedded = time_embed(timesteps[0], time_weight.shape[0])
    mod_table = jnp.dot(embedded, time_weight, precision=highest) + time_bias
    modulation = jnp.dot(onehot, mod_table, precision=highest)
    sums_rows = -(-(slot_count + 1 + n_tensor) // 8) * 8
    chosen = (own_segment[None, :] == jnp.arange(sums_rows, dtype=jnp.int32)[:, None]) & (
        own_segment[None, :] < slot_count
    )
    own_embed = jnp.where(tensor_rank == 0, embedded, 0.0)
    up_bias_rel = jnp.stack(
        [lax.dynamic_slice_in_dim(up_bias, ranks[d] * units, units)[None] for d in range(n_tensor)]
    )
    cos, sin = rope_tables(positions)
    seg_row = segment[None, :]
    seg_col = segment[:, None]

    queries, keys, values = project(normed_full, qkv_full.T, cos, sin, heads)
    mixed, log_totals = attend(queries, keys, values, seg_row, seg_col, lo, hi)

    def rows_of(array, rank):
        return lax.dynamic_slice_in_dim(array, rank * row_count, row_count, 1)

    residual_out, hidden_grad, mixed_grad, sums, up_near, down_near, proj_near, far, proj_far = middle(
        mixed,
        proj_all,
        up_both,
        down_own,
        down_far,
        residual_in,
        out_grad,
        modulation,
        chosen.astype(F32),
        own_embed,
        proj_bias[None, :],
        up_bias_rel,
        down_bias[None, :],
    )

    qkv_grad = attend_back(
        queries, keys, values, mixed_grad, mixed, log_totals, seg_row, seg_col, cos, sin, lo, hi
    )

    proj_far = to_tensor_peer(proj_far, 2)
    far = to_tensor_peer(far, 2)

    def add(near, other):
        return (near.astype(F32) + other.astype(F32)).astype(BF)

    up_sum = add(up_near, far[0])
    down_sum = add(down_near, far[1])
    proj_sum = add(proj_near, proj_far)
    embed_width, mod_width = time_weight.shape

    qkv_part = dot(normed_full, qkv_grad, 0, 1).astype(BF)
    normed_parts = [
        dot(rows_of(qkv_grad, ranks[d]), qkv_full, 0, 1).astype(BF) for d in range(n_tensor)
    ]
    input_grad, tail, packs, grads = closing(
        normed_parts,
        (up_sum, down_sum, proj_sum, qkv_part),
        residual_in,
        hidden_grad,
        norm_gain,
        sums,
        n_dp,
    )
    all_mod = packs[:, :slot_count, :mod_width].reshape(-1, mod_width)
    all_embed = packs[:, :slot_count, mod_width : mod_width + embed_width].reshape(-1, embed_width)
    grad_time_weight = lax.dot_general(
        all_embed, all_mod, (((0,), (0,)), ((), ())), precision=highest
    )
    grad_time_bias = jnp.sum(all_mod, axis=0)
    biases = jnp.sum(packs[:, slot_count : slot_count + 1 + n_tensor], axis=0)
    grad_proj_bias = biases[0, :width_model]
    grad_down_bias = biases[0, width_model : 2 * width_model]
    grad_up_bias = biases[1:, :units].reshape(-1)
    grad_up, grad_down, grad_proj, grad_qkv = grads
    grad_down = grad_down.T
    grad_proj = grad_proj.T
    grad_qkv = grad_qkv.reshape(grad_qkv.shape[0], 3, head_width).transpose(1, 0, 2)
    return (
        residual_out,
        input_grad,
        tail[0],
        tail[1],
        grad_qkv,
        grad_proj,
        grad_proj_bias,
        grad_up,
        grad_up_bias,
        grad_down,
        grad_down_bias,
        grad_time_weight,
        grad_time_bias,
    )


def solution(mesh):
    in_specs = (
        P(("dp", "tensor"), None),
        P(("dp", "tensor"), None),
        P("dp", None),
        P("dp", None),
        P(),
        P(),
        P(None, "dp", "tensor"),
        P("tensor", "dp"),
        P(),
        P("dp", "tensor"),
        P(),
        P("tensor", "dp"),
        P(),
        P(),
        P(),
    )
    out_specs = (
        P(("dp", "tensor"), None),
        P(("dp", "tensor"), None),
        P(),
        P(),
        P(None, "dp", "tensor"),
        P("tensor", "dp"),
        P(),
        P("dp", "tensor"),
        P(),
        P("tensor", "dp"),
        P(),
        P(),
        P(),
    )

    return jax.shard_map(shards, mesh=mesh, in_specs=in_specs, out_specs=out_specs, check_vma=False)
```

profile of v0, /device:TPU:0, one launch (start us, length us, event | category | flops | bytes accessed | tf_op | source)
XLA Modules:
  0.0 339.8 jit_solution(5028251568277573709)
XLA Ops:
  0.7 1.7 reduce_sum.64
  3.0 0.8 copy.49.refs_1_
  5.2 0.7 copy.48
  5.9 1.2 add_convert_fusion.refs_0_
  7.1 68.2 %opening.1 = (bf16[2048,768]{1,0:T(8,128)(2,1)}, bf16[8,96,576]{2,1,0:T(8,128)(2,1)}, bf16[4,8,96,192]{3,2,1,0:T(8,128)(2,1)}, bf16[2,8,96,768]{3,2,1,0:T(8,128)(2,1)}, bf16[8,96,768]{2,1,0:T(8,128)(2,1)}) custom-call(bf16[512,768]{1,0:T(8,128)(2,1)} %add_convert_fusion.refs_0_, bf16[96,576]{1,0:T(8,128)(2,1)} %copy.49.refs_1_, bf16[96,192]{1,0:T(8,128)(2,1)} %bitcast.61, ...), custom_call_target="tpu_custom_call" | custom-call | bytes 67108864 | tf_op jit(solution)/shard_map/opening/pallas_call | solution.py:451
  75.7 2.2 copy.50
  78.3 1.8 multiply_sine_fusion
  83.0 5.6 %project_qkv.1 = (bf16[192,2048]{1,0:T(8,128)(2,1)}, bf16[192,2048]{1,0:T(8,128)(2,1)}, bf16[192,2048]{1,0:T(8,128)(2,1)}) custom-call(bf16[2048,768]{1,0:T(8,128)(2,1)} %get-tuple-element.39.n_ref, bf16[576,768]{1,0:T(8,128)(2,1)} %bitcast.58, f32[32,2048]{1,0:T(8,128)} %get-tuple-element.121.cos_ref, f32[32,2048]{1,0:T(8,128)} %get-tuple-element.120.sin_ref), custom_call_target="tpu_custom_call" | custom-call | flops 1811939328 | bytes 8388608 | tf_op jit(solution)/shard_map/project_qkv/pallas_call | solution.py:96
  89.3 1.3 copy.51.scol_ref
  92.4 4.2 %fusion.7.refs_7_ = f32[512,2304]{1,0:T(8,128)} fusion(f32[16,2304]{1,0:T(8,128)S(1)} %convolution_add_fusion, s32[512]{0:T(512)S(1)} %get-tuple-element.113), kind=kOutput, calls=%fused_computation.26 | convolution fusion | flops 226500608 | bytes 4868096 | tf_op jit(solution)/shard_map/dot_general | solution.py:988
  96.6 28.2 %attend.1 = (bf16[192,2048]{1,0:T(8,128)(2,1)}, f32[3,2048]{1,0:T(4,128)}) custom-call(s32[8]{0:T(128)} %get-tuple-element.125.lo_ref, s32[8]{0:T(128)} %get-tuple-element.124.hi_ref, bf16[192,2048]{1,0:T(8,128)(2,1)} %get-tuple-element.41.q_ref, bf16[192,2048]{1,0:T(8,128)(2,1)} %get-tuple-element.42.k_ref, bf16[192,2048]{1,0:T(8,128)(2,1)} %get-tuple-element.43.v_ref, ...), custom_call_target="tpu_custom_call" | custom-call | flops 6442450944 | bytes 8388608 | tf_op jit(solution)/shard_map/attend/pallas_call | solution.py:166
  124.8 63.1 %middle.1 = (f32[512,768]{1,0:T(8,128)}, f32[512,768]{1,0:T(8,128)}, bf16[192,2048]{1,0:T(8,128)(2,1)}, f32[24,2560]{1,0:T(8,128)}, bf16[768,768]{1,0:T(8,128)(2...) custom-call(bf16[192,2048]{1,0:T(8,128)(2,1)} %get-tuple-element.44., ...), custom_call_target="tpu_custom_call" | custom-call | flops 14495514624 | bytes 67108864 | tf_op jit(solution)/shard_map/middle/pallas_call | solution.py:877
  187.9 1.0 collective-permute-start.2
  188.9 1.1 collective-permute-start.1
  190.0 33.5 %attend_back.1 = bf16[576,2048]{1,0:T(8,128)(2,1)} custom-call(s32[8]{0:T(128)} %get-tuple-element.125.lo_ref, s32[8]{0:T(128)} %get-tuple-element.124.hi_ref, bf16[192,2048]{1,0:T(8,128)(2,1)} %get-tuple-element.41.q_ref, bf16[192,2048]{1,0:T(8,128)(2,1)} %get-tuple-element.42.k_ref, bf16[192,2048]{1,0:T(8,128)(2,1)} %get-tuple-element.43.v_ref, ...), custom_call_target="tpu_custom_call" | custom-call | flops 16106127360 | bytes 8388608 | tf_op jit(solution)/shard_map/attend_back/pallas_call | solution.py:290
  223.5 2.9 convolution_convert_fusion.4.refs_0_
  226.4 2.9 convolution_convert_fusion.1.refs_3_
  229.3 2.9 convolution_convert_fusion
  232.3 1.8 convolution_convert_fusion.2.refs_2_
  234.0 2.2 copy.53
  236.2 2.9 convolution_convert_fusion.3.refs_1_
  239.2 1.9 add_convert_fusion.1
  241.1 8.8 %collective-permute-done.1 = bf16[2,768,768]{2,1,0:T(8,128)(2,1)S(1)} collective-permute-done((bf16[2,768,768]{2,1,0:T(8,128)(2,1)}, bf16[2,768,768]{2,1,0:T(8,128)(2,1)S(1)}, u32[]{:S(2)}, u32[]{:S(2)}) %collective-permute-start.1) | collective-permute-done | bytes 2359328 | tf_op jit(solution)/shard_map/ppermute | solution.py:930
  249.9 2.0 fusion
  251.8 75.4 %closing.1 = (f32[512,768]{1,0:T(8,128)}, f32[1,1536]{1,0:T(1,128)}, f32[8,24,2560]{2,1,0:T(8,128)}, f32[96,768]{1,0:T(8,128)}, f32[96,768]{1,0:T(8,128)}, /*index=5*/f32[96,192]{1,0:T(8,128)}, f32[96,576]{1,0:T(8,128)}) custom-call(bf16[512,768]{1,0:T(8,128)(2,1)} %convolution_convert_fusion.4.refs_0_, bf16[512,768]{1,0:T(8,128)(2,1)} %convolution_convert_fusion.3.refs_1_, ...), custom_call_target="tpu_custom_call" | custom-call | bytes 67108864 | tf_op jit(solution)/shard_map/closing/pallas_call | solution.py:598
  327.3 3.6 %convolution_bitcast_fusion = f32[128,2304]{1,0:T(8,128)} fusion(f32[8,24,2560]{2,1,0:T(8,128)} %get-tuple-element.62), kind=kOutput, calls=%fused_computation | convolution fusion | flops 452984832 | bytes 2424832 | tf_op jit(solution)/shard_map/dot_general | solution.py:1053
  332.4 0.9 copy.55
  333.9 0.7 copy.56
  335.2 1.1 copy.61
  336.4 0.8 copy-done.3
  337.2 1.1 copy.62
  339.1 0.7 copy.64
  (101 shorter events, 11.4 us)
Async XLA Ops:
  0.6 1.9 copy-start
  0.7 2.2 copy-start.9
  2.4 1.5 copy-start.10
  2.4 2.1 copy-start.11
  2.5 2.7 copy-start.15
  2.5 3.4 copy-start.19
  2.5 3.4 copy-start.23
  5.9 69.6 %copy-start.18 = (f32[3072]{0:T(1024)S(1)}, f32[3072]{0:T(1024)}, u32[]{:S(2)}) copy-start(f32[3072]{0:T(1024)} %param.25) | copy-start | bytes 36868
  7.1 70.8 %copy-start.22 = (s32[1,16]{1,0:T(1,128)S(1)}, s32[1,16]{1,0:T(1,128)}, u32[]{:S(2)}) copy-start(s32[1,16]{1,0:T(1,128)} %param.17) | copy-start | bytes 196
  7.1 71.2 %copy-start.27 = (s32[1,16]{1,0:T(1,128)S(1)}, s32[1,16]{1,0:T(1,128)}, u32[]{:S(2)}) copy-start(s32[1,16]{1,0:T(1,128)} %param.18) | copy-start | bytes 196
  75.3 6.3 %copy-start.6 = (f32[128,2304]{1,0:T(8,128)S(1)}, f32[128,2304]{1,0:T(8,128)}, u32[]{:S(2)}) copy-start(f32[128,2304]{1,0:T(8,128)} %param.28) | copy-start | bytes 3538948
  75.4 6.3 %copy-start.20 = (f32[2304]{0:T(1024)S(1)}, f32[2304]{0:T(1024)}, u32[]{:S(2)}) copy-start(f32[2304]{0:T(1024)} %param.29) | copy-start | bytes 27652
  75.4 49.4 %collective-permute-start = (bf16[768,768]{1,0:T(8,128)(2,1)}, bf16[768,768]{1,0:T(8,128)(2,1)}, u32[]{:S(2)}, u32[]{:S(2)}) collective-permute-start(bf16[768,768]{1,0:T(8,128)(2,1)} %bitcast.71), channel_id=1, source_target_pairs={{0,2},{1,3},{2,0},{3,1},{4,6},{5,7},{6,4},{7,5},{8,10},{9,11},{10,... | collective-permute-start | bytes 3538952 | tf_op jit(solution)/shard_map/ppermute | solution.py:930
  78.3 11.0 %copy-start.17 = (s32[2048]{0:T(1024)}, s32[2048]{0:T(1024)S(1)}, u32[]{:S(2)}) copy-start(s32[2048]{0:T(1024)S(1)} %get-tuple-element.108) | copy-start | bytes 24580
  83.0 7.6 %copy-start.24 = (f32[768]{0:T(1024)S(1)}, f32[768]{0:T(1024)}, u32[]{:S(2)}) copy-start(f32[768]{0:T(1024)} %param.23) | copy-start | bytes 9220
  83.0 8.2 %copy-start.25 = (f32[768]{0:T(1024)S(1)}, f32[768]{0:T(1024)}, u32[]{:S(2)}) copy-start(f32[768]{0:T(1024)} %param.27) | copy-start | bytes 9220
  187.9 51.3 %collective-permute-start.2 = (bf16[768,192]{1,0:T(8,128)(2,1)}, bf16[768,192]{1,0:T(8,128)(2,1)}, u32[]{:S(2)}, u32[]{:S(2)}) collective-permute-start(bf16[768,192]{1,0:T(8,128)(2,1)} %get-tuple-element.55), channel_id=1, source_target_pairs={{0,2},{1,3},{2,0},{3,1},{4,6},{5,7},{6,4},{7,5},{8,10},{9,11},{10,... | collective-permute-start | bytes 884744 | tf_op jit(solution)/shard_map/ppermute | solution.py:930
  188.9 60.9 %collective-permute-start.1 = (bf16[2,768,768]{2,1,0:T(8,128)(2,1)}, bf16[2,768,768]{2,1,0:T(8,128)(2,1)S(1)}, u32[]{:S(2)}, u32[]{:S(2)}) collective-permute-start(bf16[2,768,768]{2,1,0:T(8,128)(2,1)} %get-tuple-element.52), channel_id=1, source_target_pairs={{0,2},{1,3},{2,0},{3,1},{4,6},{5,7},{6,4},{7,5},{8,10},{9,11},{10,... | collective-permute-start | bytes 7077896 | tf_op jit(solution)/shard_map/ppermute | solution.py:930
  190.0 33.5 %copy-start.7 = (bf16[8,96,576]{2,1,0:T(8,128)(2,1)S(1)}, bf16[8,96,576]{2,1,0:T(8,128)(2,1)}, u32[]{:S(2)}) copy-start(bf16[8,96,576]{2,1,0:T(8,128)(2,1)} %get-tuple-element.40) | copy-start | bytes 2654212
  223.5 5.9 %copy-start.26 = (bf16[2048,768]{1,0:T(8,128)(2,1)S(1)}, bf16[2048,768]{1,0:T(8,128)(2,1)}, u32[]{:S(2)}) copy-start(bf16[2048,768]{1,0:T(8,128)(2,1)} %get-tuple-element.39.n_ref) | copy-start | bytes 9437188
  226.4 2.9 copy-start.28
  236.2 3.0 copy-start.8
  236.2 13.6 %copy-start.4 = (bf16[768,768]{1,0:T(8,128)(2,1)S(1)}, bf16[768,768]{1,0:T(8,128)(2,1)}, u32[]{:S(2)}) copy-start(bf16[768,768]{1,0:T(8,128)(2,1)} %get-tuple-element.51) | copy-start | bytes 3538948
  236.2 13.6 %copy-start.5 = (bf16[768,768]{1,0:T(8,128)(2,1)S(1)}, bf16[768,768]{1,0:T(8,128)(2,1)}, u32[]{:S(2)}) copy-start(bf16[768,768]{1,0:T(8,128)(2,1)} %get-tuple-element.53) | copy-start | bytes 3538948
  327.2 3.6 %copy-start.1 = (f32[8,24,2560]{2,1,0:T(8,128)S(1)}, f32[8,24,2560]{2,1,0:T(8,128)}, u32[]{:S(2)}) copy-start(f32[8,24,2560]{2,1,0:T(8,128)} %get-tuple-element.62) | copy-start | bytes 5898244
  330.9 1.4 copy-start.14
  330.9 3.0 copy-start.16
  330.9 3.7 %copy-start.21 = (f32[1,1536]{1,0:T(1,128)S(1)}, f32[1,1536]{1,0:T(1,128)}, u32[]{:S(2)}) copy-start(f32[1,1536]{1,0:T(1,128)} %get-tuple-element.59) | copy-start | bytes 18436
  330.9 4.4 %copy-start.2 = (f32[512,768]{1,0:T(8,128)S(1)}, f32[512,768]{1,0:T(8,128)}, u32[]{:S(2)}) copy-start(f32[512,768]{1,0:T(8,128)} %get-tuple-element.139) | copy-start | bytes 4718596
  335.2 2.0 copy-start.3
  337.2 1.1 copy-start.13
  337.2 1.9 copy-start.12
where the time goes:
time: 340 us
  Pallas kernels  274 us (81%)
  matrix products  21.9 us (6%)
  local copies, waits for them, and re-layouts  17.8 us (5%)
  other arithmetic  14.1 us (4%)
  waiting for transfers between devices  8.81 us (3%)
    pallas_call x1, Pallas kernels, closing(): pl.pallas_call(functools.partial(closing_kernel, n_z, count), name='closi...  75.4 us
    pallas_call x1, Pallas kernels, opening(): pl.pallas_call(functools.partial(opening_kernel, n_z, count), name='openi...  68.2 us
    pallas_call x1, Pallas kernels, middle(): pl.pallas_call(functools.partial(middle_kernel, 1), name='middle', in_spe...  63.1 us
    pallas_call x1, Pallas kernels, attend_back(): pl.pallas_call(functools.partial(attend_back_kernel, heads), name='attend...  33.5 us
    pallas_call x1, Pallas kernels, attend(): pl.pallas_call(functools.partial(attend_kernel, heads), name='attend', gr...  28.2 us
    dot_general x5, matrix products, dot(): lax.dot_general(a, b, (((ca,), (cb,)), ((), ())), preferred_element_type=...  13.5 us
    ppermute x3, waiting for transfers between devices, to_tensor_peer(): lax.ppermute(value, 'tensor', [(r, r ^ distance) for r in range(size)])  8.81 us
    unnamed x65, local copies, waits for them, and re-layouts  7.13 us
  transfers between devices with their start and end apart: 3, of which 1 were waited for; matrix products, arithmetic and copies ran while one was open for 10% of the time, Pallas kernels for 20%

commit v1 on v0

--- a/solution.py
+++ b/solution.py
@@ -11,8 +11,10 @@
 
 HDIM = 64
 HALF = HDIM // 2
-BQ = 256
-BK = 256
+BQ = 512
+BK = 512
+ROWS = 128
+STRIP = 256
 NEG = -1000000000.0
 MESH = pl.DeviceIdType.MESH
 BF = jnp.bfloat16
@@ -72,9 +74,14 @@
     return (jnp.cos(angles), jnp.sin(angles))
 
 
-def project_kernel(heads, n_ref, w_ref, cos_ref, sin_ref, q_ref, k_ref, v_ref):
+def project_kernel(heads, n_ref, w_ref, cos_ref, sin_ref, q_ref, k_ref, v_ref, wt_ref):
     width = heads * HDIM
-    raw = dot(w_ref[...], n_ref[...], 1, 1)
+
+    @pl.when(pl.program_id(0) == 0)
+    def _():
+        wt_ref[...] = w_ref[...].T
+
+    raw = dot(wt_ref[...], n_ref[...], 1, 1)
     cos = cos_ref[...]
     sin = sin_ref[...]
     for part, out_ref, factor in ((0, q_ref, 1.0 / math.sqrt(HDIM)), (1, k_ref, 1.0)):
@@ -87,7 +94,7 @@
     v_ref[...] = raw[2 * width :].astype(BF)
 
 
-def project(normed, weight_t, cos, sin, heads):
+def project(normed, weight, cos, sin, heads):
     rows, width_model = normed.shape
     width = heads * HDIM
     tile = 512
@@ -99,16 +106,17 @@
         grid=(rows // tile,),
         in_specs=[
             pl.BlockSpec((tile, width_model), lambda i: (i, 0)),
-            pl.BlockSpec((3 * width, width_model), lambda i: (0, 0)),
+            pl.BlockSpec((width_model, 3 * width), lambda i: (0, 0)),
             pl.BlockSpec((HALF, tile), lambda i: (0, i)),
             pl.BlockSpec((HALF, tile), lambda i: (0, i)),
         ],
         out_specs=[spec, spec, spec],
         out_shape=[out, out, out],
+        scratch_shapes=[pltpu.VMEM((3 * width, width_model), BF)],
         cost_estimate=pl.CostEstimate(
             flops=2 * rows * width_model * 3 * width, bytes_accessed=8 << 20, transcendentals=0
         ),
-    )(normed, weight_t, cos, sin)
+    )(normed, weight, cos, sin)
 
 
 def wide(column, lanes):
@@ -369,12 +377,13 @@
 
 
 def opening_kernel(n_z, count, *refs):
-    n_ref, w_refs = refs[0], refs[1 : 1 + count]
-    n_out, w_outs = refs[1 + count], refs[2 + count : 2 + 2 * count]
-    local_sem, send_sem, recv_sem = refs[2 + 2 * count :]
+    x_ref, gain_ref, bias_ref, sel_ref, table_ref = refs[:5]
+    w_refs = refs[5 : 5 + count]
+    n_out, mod_out, w_outs = refs[5 + count], refs[6 + count], refs[7 + count : 7 + 2 * count]
+    n_ref, mod_s, local_sem, send_sem, recv_sem = refs[7 + 2 * count :]
     links = Links(send_sem, recv_sem, n_z)
     greet([links.core, links.across, links.beside] + [links.along(k) for k in range(1, n_z)])
-    rows = n_ref.shape[0]
+    rows = x_ref.shape[0]
 
     def n_at(rank):
         return n_out.at[pl.ds(pl.multiple_of(rank * rows, rows), rows)]
@@ -387,17 +396,39 @@
     def cross(rank):
         crossed.append(links.send(w_outs[2].at[0, rank], w_outs[2].at[1, rank], links.across))
 
-    n_y = links.send(n_ref, n_at(links.t), links.across)
+    def norm_step(i, carry):
+        here = pl.ds(pl.multiple_of(i * ROWS, ROWS), ROWS)
+        normed, _ = normalize(x_ref[here, :])
+        n_ref[here, :] = (normed * gain_ref[...] + bias_ref[...]).astype(BF)
+        return carry
+
+    def mod_step(i):
+        here = pl.ds(i * ROWS, ROWS)
+        mod_s[here, :] = lax.dot_general(
+            sel_ref[here, :],
+            table_ref[...],
+            (((1,), (0,)), ((), ())),
+            precision=highest,
+            preferred_element_type=F32,
+        )
+        copy = pltpu.make_async_copy(mod_s.at[here], mod_out.at[here], local_sem.at[1 + count + i])
+        copy.start()
+        return copy
+
     near, far = [], []
     for n in range(count):
         near.append([links.send(w_refs[n], w_at(n, links.dp), links.along(k)) for k in range(1, n_z)])
         far.append([links.send(w_refs[n], w_at(n, links.dp), links.beside)])
-    n_core = links.send(n_ref, n_at(links.t), links.core)
+    lax.fori_loop(0, rows // ROWS, norm_step, 0)
+    tiles = rows // ROWS
+    mod_copies = []
     local = [pltpu.make_async_copy(n_ref, n_at(links.t), local_sem.at[0])]
     for n in range(count):
         local.append(pltpu.make_async_copy(w_refs[n], w_at(n, links.dp), local_sem.at[1 + n]))
     for copy in local:
         copy.start()
+    n_y = links.send(n_ref, n_at(links.t), links.across)
+    n_core = links.send(n_ref, n_at(links.t), links.core)
     others = []
     for n in range(count):
         for k in range(1, n_z):
@@ -406,6 +437,9 @@
             far[n].append(links.send(w_at(n, rank), w_at(n, rank), links.beside))
             if n == 2:
                 cross(rank)
+        if n < 2:
+            for i in range(n * tiles // 2, (n + 1) * tiles // 2):
+                mod_copies.append(mod_step(i))
         if n == 2:
             local[1 + n].wait()
             cross(links.dp)
@@ -437,11 +471,12 @@
         copy.wait_recv()
     for copy in [n_y, n_core, n_relay] + others + crossed:
         copy.wait_send()
-    local[0].wait()
-
-
-def opening(normed, weights, n_dp, n_tensor):
-    rows, width = normed.shape
+    for copy in local[:1] + mod_copies:
+        copy.wait()
+
+
+def opening(x, gain, bias, sel, table, weights, n_dp, n_tensor):
+    rows, width = x.shape
     n_z = n_dp // 2
     count = len(weights)
     slots = count * (2 * n_z - 1) + 6 + n_dp
@@ -451,104 +486,148 @@
     return pl.pallas_call(
         functools.partial(opening_kernel, n_z, count),
         name="opening",
-        in_specs=[pl.BlockSpec(memory_space=pltpu.VMEM)] * (1 + count),
-        out_specs=[pl.BlockSpec(memory_space=pl.ANY)] * (1 + count),
-        out_shape=[jax.ShapeDtypeStruct((n_tensor * rows, width), BF)]
+        in_specs=[pl.BlockSpec(memory_space=pltpu.VMEM)] * (5 + count),
+        out_specs=[pl.BlockSpec(memory_space=pl.ANY)] * (2 + count),
+        out_shape=[
+            jax.ShapeDtypeStruct((n_tensor * rows, width), BF),
+            jax.ShapeDtypeStruct((rows, table.shape[1]), F32),
+        ]
         + [jax.ShapeDtypeStruct(shape, BF) for shape in shapes],
         scratch_shapes=[
-            pltpu.SemaphoreType.DMA((1 + count,)),
+            pltpu.VMEM((rows, width), BF),
+            pltpu.VMEM((rows, table.shape[1]), F32),
+            pltpu.SemaphoreType.DMA((1 + count + rows // ROWS,)),
             pltpu.SemaphoreType.DMA((slots,)),
             pltpu.SemaphoreType.DMA((slots,)),
         ],
-        compiler_params=pltpu.CompilerParams(collective_id=0, has_side_effects=True),
+        compiler_params=pltpu.CompilerParams(
+            collective_id=0, has_side_effects=True, vmem_limit_bytes=VMEM_LIMIT
+        ),
         cost_estimate=pl.CostEstimate(flops=0, bytes_accessed=64 << 20, transcendentals=0),
-    )(normed, *weights)
-
-
-def closing_kernel(n_z, count, *refs):
-    part_refs = refs[:4]
-    w_refs = refs[4 : 4 + count]
-    x_ref, h_ref, gain_ref, sums_ref = refs[4 + count : 8 + count]
-    outs = refs[8 + count : 11 + 2 * count]
-    in_grad_ref, tail_ref, all_ref, g_refs = outs[0], outs[1], outs[2], outs[3:]
-    scratch = refs[11 + 2 * count :]
-    core_buf, y_send, y_recv, vec, all_vec, sums_buf = scratch[:6]
-    x_recv = scratch[6 : 6 + count]
-    z_send = scratch[6 + count : 6 + 2 * count]
-    z_recv = scratch[6 + 2 * count : 6 + 3 * count]
-    send_sem, recv_sem = scratch[6 + 3 * count :]
+    )(x, gain[None, :], bias[None, :], sel, table, *weights)
+
+
+def closing_kernel(n_z, *refs):
+    g_ref, n_ref, w_ref, up_keep, up_got, down_near, down_far, proj_near, proj_far = refs[:9]
+    x_ref, h_ref, gain_ref, sums_ref = refs[9:13]
+    in_grad_ref, tail_ref, all_ref, up_out, down_out, proj_out, qkv_out = refs[13:20]
+    part_send, core_buf, y_send, y_recv, vec, all_vec, qkv_flat, qkv_ref = refs[20:28]
+    up_y_send, up_y_recv = refs[28:30]
+    x_send, x_recv = refs[30:32], refs[32:35]
+    z_send, z_recv = refs[35:39], refs[39:43]
+    send_sem, recv_sem = refs[43:]
     links = Links(send_sem, recv_sem, n_z)
+    z, x = links.z, links.x
     n_dp = 2 * n_z
+    rows, width = x_ref.shape
+    outs = (up_out, down_out, proj_out, qkv_out)
+    pairs = (None, (down_near, down_far), (proj_near, proj_far))
     dp_peers = [{"dp": (links.dp + k) % n_dp} for k in range(1, n_dp)]
     diagonal = {"tensor": 3 - links.t}
+    ranks = [links.t, links.core_rank, links.y_rank, 3 - links.t]
     greet([links.core, links.across, diagonal] + dp_peers)
 
-    c1 = links.send(part_refs[1], core_buf.at[0], links.core)
-    c3 = links.send(part_refs[3], core_buf.at[1], links.core)
-    quarter = sums_ref.shape[1] // 4
+    quarter = sums_ref.shape[2]
 
     def lanes(rank):
         return pl.ds(pl.multiple_of(rank * quarter, 128), quarter)
 
-    ranks = (links.core_rank, links.y_rank, 3 - links.t)
-    tensor_peers = (links.core, links.across, diagonal)
-    sums_tensor = [
-        links.send(sums_ref.at[:, lanes(rank)], sums_buf.at[links.t], peer)
-        for rank, peer in zip(ranks, tensor_peers)
-    ]
-    sums_buf[links.t] = sums_ref[:, lanes(links.t)]
-    x_slots = [links.slots(n_z) for _ in range(count)]
-    z_slots = [links.slots(n_z) for _ in range(count)]
+    own_lanes = lanes(links.t)
+    all_ref[:, :, own_lanes] = sums_ref[...]
+    up_slots = links.slots(n_z)
+    x_slots = [None] + [links.slots(n_z) for _ in range(3)]
+    z_slots = [links.slots(n_z) for _ in range(4)]
+    order = list(range(1, n_z)) + [0]
+
+    def at(s):
+        return (z + s) % n_z
+
+    def up_copy(s):
+        return links.copy(up_y_send.at[s], up_y_recv.at[s], links.across, up_slots + s)
 
     def x_copy(n, s):
-        target = (links.z + s) % n_z
-        src = w_refs[n].at[target, 1 - links.x]
-        return links.copy(src, x_recv[n].at[s], links.beside, x_slots[n] + s)
+        src = qkv_ref.at[at(s), 1 - x] if n == 3 else x_send[n - 1].at[s]
+        return links.copy(src, x_recv[n - 1].at[s], links.beside, x_slots[n] + s)
 
     def z_copy(n, s):
-        peer = {"dp": 2 * ((links.z + s) % n_z) + links.x}
+        peer = {"dp": 2 * at(s) + x}
         return links.copy(z_send[n].at[s], z_recv[n].at[s], peer, z_slots[n] + s)
 
-    def x_sum(n, s):
+    def both(n, s, side):
+        near, far = pairs[n]
+        return near[at(s), side].astype(F32) + far[at(s), side].astype(F32)
+
+    def x_start(n):
+        for s in order:
+            if n < 3:
+                x_send[n - 1][s] = both(n, s, 1 - x).astype(BF)
+            x_copy(n, s).start()
+
+    def value(n, s):
+        if n == 0:
+            up_copy(s).wait_recv()
+            own = up_keep[0, at(s)].astype(F32) + up_got[0, at(s)].astype(F32)
+            return own + up_y_recv[s].astype(F32)
         x_copy(n, s).wait_recv()
-        own = w_refs[n][(links.z + s) % n_z, links.x]
-        return own.astype(F32) + x_recv[n][s].astype(F32)
-
-    for n in range(count):
-        for s in list(range(1, n_z)) + [0]:
-            x_copy(n, s).start()
-
-    c1.wait_recv()
+        own = qkv_ref[at(s), x].astype(F32) if n == 3 else both(n, s, x)
+        return own + x_recv[n - 1][s].astype(F32)
+
+    def z_start(n):
+        for s in range(1, n_z):
+            z_send[n][s] = value(n, s).astype(BF)
+            z_copy(n, s).start()
+        outs[n][...] = value(n, 0)
+
+    def finish(n):
+        for s in range(1, n_z):
+            z_copy(n, s).wait_recv()
+            outs[n][...] += z_recv[n][s].astype(F32)
+
+    def part(d):
+        here = pl.ds(pl.multiple_of(ranks[d] * rows, rows), rows)
+        return dot(g_ref[:, here].T, w_ref[...], 1, 1)
+
+    x_start(1)
+    for s in order:
+        up_y_send[s] = (up_keep[1, at(s)].astype(F32) + up_got[1, at(s)].astype(F32)).astype(BF)
+        up_copy(s).start()
+    x_start(2)
+    part_send[0] = part(3).astype(BF)
+    part_send[1] = part(1).astype(BF)
+    c3 = links.send(part_send.at[0], core_buf.at[0], links.core)
+    z_start(1)
+    c1 = links.send(part_send.at[1], core_buf.at[1], links.core)
+    far = part(2)
     c3.wait_recv()
-    y_send[...] = (part_refs[2][...].astype(F32) + core_buf[1].astype(F32)).astype(BF)
-    for copy in sums_tensor:
-        copy.wait_recv()
-    own_lanes = lanes(links.t)
-    all_ref[links.dp, :, own_lanes] = sums_buf[0] + sums_buf[1] + sums_buf[2] + sums_buf[3]
-    late = None
-    y_copy = links.copy(y_send, y_recv, links.across, links.slots(1))
-    started = False
-    for n in range(count):
-        for s in range(1, n_z):
-            z_send[n][s] = x_sum(n, s).astype(BF)
-            if not started:
-                y_copy.start()
-                started = True
-                here = all_ref.at[links.dp, :, own_lanes]
-                sums_dp = [links.send(here, here, peer) for peer in dp_peers]
-            if late is not None:
-                z_copy(*late).start()
-            late = (n, s)
-        g_refs[n][...] = x_sum(n, 0)
-    z_copy(*late).start()
-
-    for copy in sums_dp:
-        copy.wait_recv()
+    y_send[...] = (far + core_buf[0].astype(F32)).astype(BF)
+
+    strip = 256
+
+    def qkv_step(j, carry):
+        here = pl.ds(pl.multiple_of(j * strip, strip), strip)
+        qkv_flat[here, :] = dot(g_ref[...], n_ref[:, here], 1, 0).T.astype(BF)
+        return carry
+
+    y_copy = links.send(y_send, y_recv, links.across)
     here = all_ref.at[:, :, own_lanes]
     there = all_ref.at[:, :, lanes(links.y_rank)]
-    sums_last = [links.send(here, here, links.across), links.send(here, here, links.core)]
+    sums_last = [
+        links.send(sums_ref, here, links.across),
+        links.send(sums_ref, here, links.core),
+    ]
+    lax.fori_loop(0, width // strip, qkv_step, 0)
+    depth = qkv_ref.shape[2]
+    for r in range(n_dp):
+        qkv_ref[r // 2, r % 2] = qkv_flat[r * depth : (r + 1) * depth, :]
+    z_start(0)
+    x_start(3)
+    z_start(2)
+    near = part(0)
+    c1.wait_recv()
+    near = near + core_buf[1].astype(F32)
+    z_start(3)
     y_copy.wait_recv()
-    grad = part_refs[0][...].astype(F32) + core_buf[0].astype(F32) + y_recv[...].astype(F32)
+    grad = near + y_recv[...].astype(F32)
     normed, inverse = normalize(x_ref[...])
     own_vec = jnp.concatenate(
         [jnp.sum(grad * normed, axis=0, keepdims=True), jnp.sum(grad, axis=0, keepdims=True)], axis=1
@@ -559,17 +638,16 @@
         links.send(vec.at[links.t], vec.at[links.t], peer)
         for peer in (links.core, links.across, diagonal)
     ]
+    finish(1)
+    for copy in tensor_sends:
+        copy.wait_recv()
+    all_vec[links.dp] = vec[0] + vec[1] + vec[2] + vec[3]
+    finish(0)
+    dp_sends = [links.send(all_vec.at[links.dp], all_vec.at[links.dp], peer) for peer in dp_peers]
     sums_last[0].wait_recv()
     sums_last.append(links.send(there, there, links.core))
-    for copy in tensor_sends:
-        copy.wait()
-    total = vec[0] + vec[1] + vec[2] + vec[3]
-    all_vec[links.dp] = total
-    for n in range(count):
-        for s in range(1, n_z):
-            z_copy(n, s).wait_recv()
-            g_refs[n][...] += z_recv[n][s].astype(F32)
-    dp_sends = [links.send(all_vec.at[links.dp], all_vec.at[links.dp], peer) for peer in dp_peers]
+    finish(2)
+    finish(3)
     for copy in dp_sends:
         copy.wait_recv()
     total = all_vec[0]
@@ -578,57 +656,78 @@
     tail_ref[...] = total
     sums_last[1].wait_recv()
     sums_last[2].wait_recv()
-    for copy in [c1, c3, y_copy] + dp_sends + sums_tensor + sums_dp + sums_last:
+    for copy in [c1, c3, y_copy] + dp_sends + sums_last + tensor_sends:
         copy.wait_send()
-    for n in range(count):
-        for s in range(n_z):
-            x_copy(n, s).wait_send()
+    for s in range(n_z):
+        up_copy(s).wait_send()
+        for n in range(4):
+            if n > 0:
+                x_copy(n, s).wait_send()
             if s > 0:
                 z_copy(n, s).wait_send()
 
 
-def closing(parts, weights, residual_in, hidden_grad, gain, sums, n_dp):
+def closing(qkv_grad, normed, weight, up, down, proj, residual_in, hidden_grad, gain, sums, n_dp):
     rows, width = residual_in.shape
+    head_width = weight.shape[1]
     n_z = n_dp // 2
-    count = len(weights)
-    blocks = [w.reshape(n_z, 2, w.shape[0] // n_dp, w.shape[1]) for w in weights]
-    shards = [b.shape[2:] for b in blocks]
-    slots = 2 + 2 * count * n_z + 1 + 3 + (n_dp - 1) + 3 + (n_dp - 1) + 3
+    depth = width // n_dp
+
+    def blocks(pair):
+        return [w.reshape(n_z, 2, depth, w.shape[-1]) for w in pair]
+
+    columns = [up[0].shape[-1], down[0].shape[-1], proj[0].shape[-1], head_width]
+    shards = [(depth, c) for c in columns]
+    stacks = [(n_z,) + shard for shard in shards]
+    slots = 8 * n_z + 2 + 1 + 3 + 3 + (n_dp - 1)
     vmem = pl.BlockSpec(memory_space=pltpu.VMEM)
     out = pl.pallas_call(
-        functools.partial(closing_kernel, n_z, count),
+        functools.partial(closing_kernel, n_z),
         name="closing",
-        in_specs=[vmem] * (8 + count),
-        out_specs=[vmem] * (3 + count),
+        in_specs=[vmem] * 13,
+        out_specs=[vmem] * 7,
         out_shape=[
             jax.ShapeDtypeStruct((rows, width), F32),
             jax.ShapeDtypeStruct((1, 2 * width), F32),
-            jax.ShapeDtypeStruct((n_dp,) + sums.shape, F32),
+            jax.ShapeDtypeStruct(sums.shape[:2] + (4 * sums.shape[2],), F32),
         ]
         + [jax.ShapeDtypeStruct(shape, F32) for shape in shards],
         scratch_shapes=[
+            pltpu.VMEM((2, rows, width), BF),
             pltpu.VMEM((2, rows, width), BF),
             pltpu.VMEM((rows, width), BF),
             pltpu.VMEM((rows, width), BF),
             pltpu.VMEM((4, 1, 2 * width), F32),
             pltpu.VMEM((n_dp, 1, 2 * width), F32),
-            pltpu.VMEM((4, sums.shape[0], sums.shape[1] // 4), F32),
+            pltpu.VMEM((width, head_width), BF),
+            pltpu.VMEM((n_z, 2) + shards[3], BF),
+            pltpu.VMEM(stacks[0], BF),
+            pltpu.VMEM(stacks[0], BF),
         ]
-        + [pltpu.VMEM((n_z,) + shape, BF) for _ in range(3) for shape in shards]
+        + [pltpu.VMEM(shape, BF) for shape in stacks[1:3]]
+        + [pltpu.VMEM(shape, BF) for shape in stacks[1:]]
+        + [pltpu.VMEM(shape, BF) for _ in range(2) for shape in stacks]
         + [pltpu.SemaphoreType.DMA((slots,)), pltpu.SemaphoreType.DMA((slots,))],
         compiler_params=pltpu.CompilerParams(
             collective_id=1, has_side_effects=True, vmem_limit_bytes=VMEM_LIMIT
         ),
         cost_estimate=pl.CostEstimate(flops=0, bytes_accessed=64 << 20, transcendentals=0),
-    )(*parts, *blocks, residual_in, hidden_grad, gain[None, :], sums)
+    )(
+        qkv_grad,
+        normed,
+        weight,
+        *up,
+        *blocks(down),
+        *blocks(proj),
+        residual_in,
+        hidden_grad,
+        gain[None, :],
+        sums,
+    )
     return out[0], out[1].reshape(2, width), out[2], out[3:]
 
 
-ROWS = 128
-STRIP = 256
-
-
-def middle_kernel(slots, *refs):
+def middle_kernel(n_z, *refs):
     (
         mixed_ref,
         proj_ref,
@@ -644,9 +743,8 @@
         up_bias_ref,
         down_bias_ref,
     ) = refs[:13]
-    out_ref, h_grad_ref, mixed_grad_ref, sums_ref, up_near, down_near, proj_near, far, proj_far = refs[
-        13:22
-    ]
+    out_ref, h_grad_ref, mixed_grad_ref, packs_ref, down_near, proj_near, down_far, proj_far = refs[13:21]
+    up_keep, up_away = refs[21:23]
     (
         mix_buf,
         mix_t,
@@ -669,15 +767,21 @@
         back_s,
         proj_send,
         proj_recv,
+        sums_ref,
+        sums_buf,
         local_sem,
         send_sem,
         recv_sem,
-    ) = refs[22:]
-    links = Links(send_sem, recv_sem, slots)
+    ) = refs[23:]
+    links = Links(send_sem, recv_sem, n_z)
+    depth = up_keep.shape[2]
     rows, width = x_ref.shape
     peers = [None, links.core, links.across, {"tensor": 3 - links.t}]
     ranks = [links.t, links.core_rank, links.y_rank, 3 - links.t]
-    greet(peers[1:])
+    n_dp = 2 * n_z
+    dp_peers = [{"dp": (links.dp + k) % n_dp} for k in range(1, n_dp)]
+    greet(peers[1:] + dp_peers)
+    quarter = sums_ref.shape[1] // 4
 
     def lanes(rank):
         return pl.ds(pl.multiple_of(rank * rows, rows), rows)
@@ -800,16 +904,27 @@
     for copy in local:
         copy.wait()
 
-    for e, up_out, down_out in ((1, far.at[0], far.at[1]), (0, up_near, down_near)):
+    for e, down_sum in ((1, down_far), (0, down_near)):
         feed(2 * e)
         up_copy(e).wait_recv()
         down_copy(e).wait_recv()
 
         def store(here, up_part, down_part):
-            up_out[here, :] = (up_part + up_recv[e, here, :].astype(F32)).astype(BF)
-            down_out[here, :] = (down_part + down_recv[e, here, :].astype(F32)).astype(BF)
-
+            up_send[e, here, :] = (up_part + up_recv[e, here, :].astype(F32)).astype(BF)
+            down_sum[here, :] = (down_part + down_recv[e, here, :].astype(F32)).astype(BF)
+
+        up_copy(e).wait_send()
         grads(store)
+        for r in range(2 * n_z):
+            block = up_send[e, r * depth : (r + 1) * depth, :]
+
+            @pl.when(links.x == r % 2)
+            def _():
+                up_keep[e, r // 2] = block
+
+            @pl.when(links.x != r % 2)
+            def _():
+                up_away[e, r // 2] = block
 
     def back_step(i, total):
         here = tile(i)
@@ -832,63 +947,80 @@
         return total + jnp.sum(h_grad, axis=0, keepdims=True)
 
     proj_bias_sum = tiles(back_step, jnp.zeros((1, width), F32))
+    sums_ref[16:17, :width] = proj_bias_sum
+    sums_ref[16:17, width : 2 * width] = down_bias_sum
+    embed_at = 3 * width
+    sums_ref[: embed_ref.shape[0], embed_at : embed_at + embed_ref.shape[1]] = embed_ref[...]
+
+    def columns(rank):
+        return pl.ds(pl.multiple_of(rank * quarter, 128), quarter)
+
     back_copies = []
+    sums_copies = []
     for d in (3, 2, 1, 0):
         part = dot(low_s[...], proj_ref[d], 1, 0).astype(BF).T
         if d == 0:
             mixed_grad_ref[:, lanes(links.t)] = part
         else:
             back_s[d] = part
+            sums_copies.append(
+                links.send(sums_ref.at[:, columns(ranks[d])], sums_buf.at[links.t], peers[d])
+            )
         if d < 3:
             back_copies.append(
                 links.send(back_s.at[d + 1], mixed_grad_ref.at[:, lanes(links.t)], peers[d + 1])
             )
-    sums_ref[16:17, :width] = proj_bias_sum
-    sums_ref[16:17, width : 2 * width] = down_bias_sum
-    embed_at = 3 * width
-    sums_ref[: embed_ref.shape[0], embed_at : embed_at + embed_ref.shape[1]] = embed_ref[...]
+    sums_buf[links.t] = sums_ref[:, columns(links.t)]
     flip_s[...] = low_s[...].T
     for d in (1, 3):
         proj_send[d // 2] = dot(flip_s[...], mix_t[d], 1, 0).astype(BF)
+    for copy in sums_copies:
+        copy.wait_recv()
+    packs_ref[links.dp] = sums_buf[0] + sums_buf[1] + sums_buf[2] + sums_buf[3]
     own_part = dot(flip_s[...], mix_t[0], 1, 0)
+    here = packs_ref.at[links.dp]
+    sums_dp = [links.send(here, here, peer) for peer in dp_peers]
     proj_copies = [links.send(proj_send.at[e], proj_recv.at[e], links.core) for e in range(2)]
     far_part = dot(flip_s[...], mix_t[2], 1, 0)
     for e, part, out in ((0, own_part, proj_near), (1, far_part, proj_far)):
         proj_copies[e].wait_recv()
         out[...] = (part + proj_recv[e].astype(F32)).astype(BF)
-    for copy in back_copies:
+    for copy in back_copies + sums_dp:
         copy.wait_recv()
-    for copy in mix_copies + w_copies + back_copies + proj_copies:
+    for copy in mix_copies + w_copies + back_copies + proj_copies + sums_copies + sums_dp:
         copy.wait_send()
     for e in range(2):
-        up_copy(e).wait_send()
         down_copy(e).wait_send()
 
 
-def middle(mixed, proj, up, down, down_far, x, grad, mod, sel, embed, proj_bias, up_bias, down_bias):
+def middle(
+    mixed, proj, up, down, down_far, x, grad, mod, sel, embed, proj_bias, up_bias, down_bias, n_dp
+):
     rows, width = x.shape
     head_width, total_rows = mixed.shape
     units = down.shape[1]
     vmem = pl.BlockSpec(memory_space=pltpu.VMEM)
     hbm = pl.BlockSpec(memory_space=pl.ANY)
     sums = (sel.shape[0], -(-(3 * width + embed.shape[1]) // 512) * 512)
-    slots = 3 + 4 + 4 + 3 + 2
+    slots = 3 + 4 + 4 + 3 + 2 + 3 + (n_dp - 1)
     square = (2, width, units)
+    halves = (2, n_dp // 2, width // n_dp, units)
     return pl.pallas_call(
-        functools.partial(middle_kernel, 1),
+        functools.partial(middle_kernel, n_dp // 2),
         name="middle",
         in_specs=[vmem, vmem, hbm, hbm, hbm] + [vmem] * 8,
-        out_specs=[vmem] * 9,
+        out_specs=[vmem] * 10,
         out_shape=[
             jax.ShapeDtypeStruct((rows, width), F32),
             jax.ShapeDtypeStruct((rows, width), F32),
             jax.ShapeDtypeStruct((head_width, total_rows), BF),
-            jax.ShapeDtypeStruct(sums, F32),
-            jax.ShapeDtypeStruct(square[1:], BF),
+            jax.ShapeDtypeStruct((n_dp, sums[0], sums[1] // 4), F32),
             jax.ShapeDtypeStruct(square[1:], BF),
             jax.ShapeDtypeStruct((width, head_width), BF),
-            jax.ShapeDtypeStruct(square, BF),
+            jax.ShapeDtypeStruct(square[1:], BF),
             jax.ShapeDtypeStruct((width, head_width), BF),
+            jax.ShapeDtypeStruct(halves, BF),
+            jax.ShapeDtypeStruct(halves, BF),
         ],
         scratch_shapes=[
             pltpu.VMEM((4, head_width, rows), BF),
@@ -912,6 +1044,8 @@
             pltpu.VMEM((4, head_width, rows), BF),
             pltpu.VMEM((2, width, head_width), BF),
             pltpu.VMEM((2, width, head_width), BF),
+            pltpu.VMEM(sums, F32),
+            pltpu.VMEM((4, sums[0], sums[1] // 4), F32),
             pltpu.SemaphoreType.DMA((4,)),
             pltpu.SemaphoreType.DMA((slots,)),
             pltpu.SemaphoreType.DMA((slots,)),
@@ -958,11 +1092,28 @@
     units = up_weight.shape[1]
     ranks = [tensor_rank ^ d for d in range(n_tensor)]
 
-    normed_in, _ = normalize(residual_in)
-    normed_low = (normed_in * norm_gain + norm_bias).astype(BF)
+    segment, positions = pack_info(seq_lengths[0], total_rows)
+    lo, hi = key_ranges(seq_lengths[0], total_rows)
+    own_segment = lax.dynamic_slice_in_dim(segment, tensor_rank * row_count, row_count)
+    slots = jnp.arange(slot_count, dtype=jnp.int32)
+    onehot = (own_segment[:, None] == slots[None, :]).astype(F32)
+    embedded = time_embed(timesteps[0], time_weight.shape[0])
+    mod_table = jnp.dot(embedded, time_weight, precision=highest) + time_bias
+    sums_rows = -(-(slot_count + 1 + n_tensor) // 8) * 8
+    chosen = (own_segment[None, :] == jnp.arange(sums_rows, dtype=jnp.int32)[:, None]) & (
+        own_segment[None, :] < slot_count
+    )
+    own_embed = jnp.where(tensor_rank == 0, embedded, 0.0)
+    up_bias_rel = jnp.stack(
+        [lax.dynamic_slice_in_dim(up_bias, ranks[d] * units, units)[None] for d in range(n_tensor)]
+    )
     qkv_shard = jnp.transpose(qkv_weight, (1, 0, 2)).reshape(qkv_weight.shape[1], -1).astype(BF)
-    normed_full, qkv_full, proj_all, up_own, down_own = opening(
-        normed_low,
+    normed_full, modulation, qkv_full, proj_all, up_own, down_own = opening(
+        residual_in,
+        norm_gain,
+        norm_bias,
+        onehot,
+        mod_table,
         (
             qkv_shard,
             proj_weight.T.astype(BF),
@@ -978,33 +1129,14 @@
     down_own = down_own.reshape(width_model, -1)
     down_far = to_tensor_peer(down_own, 2)
 
-    segment, positions = pack_info(seq_lengths[0], total_rows)
-    lo, hi = key_ranges(seq_lengths[0], total_rows)
-    own_segment = lax.dynamic_slice_in_dim(segment, tensor_rank * row_count, row_count)
-    slots = jnp.arange(slot_count, dtype=jnp.int32)
-    onehot = (own_segment[:, None] == slots[None, :]).astype(F32)
-    embedded = time_embed(timesteps[0], time_weight.shape[0])
-    mod_table = jnp.dot(embedded, time_weight, precision=highest) + time_bias
-    modulation = jnp.dot(onehot, mod_table, precision=highest)
-    sums_rows = -(-(slot_count + 1 + n_tensor) // 8) * 8
-    chosen = (own_segment[None, :] == jnp.arange(sums_rows, dtype=jnp.int32)[:, None]) & (
-        own_segment[None, :] < slot_count
-    )
-    own_embed = jnp.where(tensor_rank == 0, embedded, 0.0)
-    up_bias_rel = jnp.stack(
-        [lax.dynamic_slice_in_dim(up_bias, ranks[d] * units, units)[None] for d in range(n_tensor)]
-    )
     cos, sin = rope_tables(positions)
     seg_row = segment[None, :]
     seg_col = segment[:, None]
 
-    queries, keys, values = project(normed_full, qkv_full.T, cos, sin, heads)
+    queries, keys, values = project(normed_full, qkv_full, cos, sin, heads)
     mixed, log_totals = attend(queries, keys, values, seg_row, seg_col, lo, hi)
 
-    def rows_of(array, rank):
-        return lax.dynamic_slice_in_dim(array, rank * row_count, row_count, 1)
-
-    residual_out, hidden_grad, mixed_grad, sums, up_near, down_near, proj_near, far, proj_far = middle(
+    outs = middle(
         mixed,
         proj_all,
         up_both,
@@ -1018,30 +1150,27 @@
         proj_bias[None, :],
         up_bias_rel,
         down_bias[None, :],
-    )
+        n_dp,
+    )
+    residual_out, hidden_grad, mixed_grad, sums, down_near, proj_near, down_other, proj_other = outs[:8]
+    up_keep, up_away = outs[8:]
 
     qkv_grad = attend_back(
         queries, keys, values, mixed_grad, mixed, log_totals, seg_row, seg_col, cos, sin, lo, hi
     )
 
-    proj_far = to_tensor_peer(proj_far, 2)
-    far = to_tensor_peer(far, 2)
-
-    def add(near, other):
-        return (near.astype(F32) + other.astype(F32)).astype(BF)
-
-    up_sum = add(up_near, far[0])
-    down_sum = add(down_near, far[1])
-    proj_sum = add(proj_near, proj_far)
+    proj_far = to_tensor_peer(proj_other, 2)
+    down_far = to_tensor_peer(down_other, 2)
+    up_got = lax.ppermute(up_away, "dp", [(r, r ^ 1) for r in range(n_dp)])
     embed_width, mod_width = time_weight.shape
 
-    qkv_part = dot(normed_full, qkv_grad, 0, 1).astype(BF)
-    normed_parts = [
-        dot(rows_of(qkv_grad, ranks[d]), qkv_full, 0, 1).astype(BF) for d in range(n_tensor)
-    ]
     input_grad, tail, packs, grads = closing(
-        normed_parts,
-        (up_sum, down_sum, proj_sum, qkv_part),
+        qkv_grad,
+        normed_full,
+        qkv_full,
+        (up_keep, up_got),
+        (down_near, down_far),
+        (proj_near, proj_far),
         residual_in,
         hidden_grad,
         norm_gain,

time: 340 us -> 299 us (0.88)
  Pallas kernels: 274 us -> 251 us
  matrix products: 21.9 us -> 4.91 us
  waiting for transfers between devices: 8.81 us -> 4.56 us
  starting transfers between devices: 2.16 us -> 6.19 us
    dot_general x6 -> x0, matrix products: 17.7 us -> none  [the longest x5 13.5 us: dot(): lax.dot_general(a, b, (((ca,), (cb,)), ((), ())), preferred_element_type=...]
    pallas_call x1, Pallas kernels: 28.2 us -> 17.9 us  [attend(): pl.pallas_call(functools.partial(attend_kernel, heads), name='attend', gr...]
    pallas_call x1, Pallas kernels: 33.5 us -> 26.4 us  [attend_back(): pl.pallas_call(functools.partial(attend_back_kernel, heads), name='attend...]
    pallas_call x2, Pallas kernels: 138 us -> 132 us  [the longest x1 66.6 us: middle(): pl.pallas_call(functools.partial(middle_kernel, n_dp // 2), name='middle'...]
    ppermute x3, waiting for transfers between devices: 8.81 us -> 4.56 us  [to_tensor_peer(): lax.ppermute(value, 'tensor', [(r, r ^ distance) for r in range(size)])]
    convert_element_type x3 -> x1, other arithmetic: 5.02 us -> 0.84 us  [shards(): onehot = (own_segment[:, None] == slots[None, :]).astype(F32)]
    unnamed x65 -> x43, local copies, waits for them, and re-layouts: 7.13 us -> 8.85 us
  transfers between devices with their start and end apart: 3 -> 4, of which waited for: 1 -> 1; matrix products, arithmetic and copies ran while one was open for 10% -> 2% of each run, Pallas kernels for 20% -> 17%
where the time goes in v1:
time: 299 us; the launch traced here: 298 us
  Pallas kernels  251 us (84%)
  local copies, waits for them, and re-layouts  17.7 us (6%)
  other arithmetic  13.1 us (4%)
  starting transfers between devices  6.19 us (2%)
  matrix products  4.91 us (2%)
  waiting for transfers between devices  4.56 us (2%)
    pallas_call x1, Pallas kernels, opening(): pl.pallas_call(functools.partial(opening_kernel, n_z, count), name='openi...  68.6 us
    pallas_call x1, Pallas kernels, middle(): pl.pallas_call(functools.partial(middle_kernel, n_dp // 2), name='middle'...  66.6 us
    pallas_call x1, Pallas kernels, closing(): pl.pallas_call(functools.partial(closing_kernel, n_z), name='closing', in...  65.7 us
    pallas_call x1, Pallas kernels, attend_back(): pl.pallas_call(functools.partial(attend_back_kernel, heads), name='attend...  26.4 us
    pallas_call x1, Pallas kernels, attend(): pl.pallas_call(functools.partial(attend_kernel, heads), name='attend', gr...  17.9 us
    unnamed x43, local copies, waits for them, and re-layouts  8.85 us
  transfers between devices with their start and end apart: 4, of which 1 were waited for; matrix products, arithmetic and copies ran while one was open for 2% of the time, Pallas kernels for 17%

profile of v1, /device:TPU:0, one launch (start us, length us, event | category | flops | bytes accessed | tf_op | source)
XLA Modules:
  0.0 298.5 jit_solution(7497571987888043601)
XLA Ops:
  0.7 0.8 convert_bitcast_fusion.3
  1.5 1.3 broadcast_in_dim.76.refs_1_.refs_11_
  2.7 1.3 broadcast_in_dim.77.refs_2_
  4.0 0.7 copy.42
  4.9 1.6 copy.44
  6.5 1.0 convert_bitcast_fusion.1
  7.6 0.8 copy.45.refs_5_
  8.4 1.6 convert_element_type.55.refs_7_
  11.0 0.8 fusion.1.refs_3_
  12.0 1.3 convolution_add_fusion.refs_4_
  13.3 68.6 %opening.1 = (bf16[2048,768]{1,0:T(8,128)(2,1)}, f32[512,2304]{1,0:T(8,128)}, bf16[8,96,576]{2,1,0:T(8,128)(2,1)}, bf16[4,8,96,192]{3,2,1,0:T(8,128)(2,1)}, bf16...) custom-call(f32[512,768]{1,0:T(8,128)} %refs_9_.1, f32[1,768]{1,0:T(1,128)} %broadcast_in_dim.76.refs_1_.refs_11_, ...), custom_call_target="tpu_custom_call" | custom-call | bytes 67108864 | tf_op jit(solution)/shard_map/opening/pallas_call | solution.py:486
  82.9 1.8 multiply_sine_fusion
  85.3 6.0 %project_qkv.1 = (bf16[192,2048]{1,0:T(8,128)(2,1)}, bf16[192,2048]{1,0:T(8,128)(2,1)}, bf16[192,2048]{1,0:T(8,128)(2,1)}) custom-call(bf16[2048,768]{1,0:T(8,128)(2,1)} %get-tuple-element.41.n_ref.refs_1_, bf16[768,576]{1,0:T(8,128)(2,1)} %bitcast.33, f32[32,2048]{1,0:T(8,128)} %get-tuple-element.123.cos_ref, f32[32,2048]{1,0:T(8,128)} %get-tuple-element.122.sin_ref), custom_call_target="tpu_custom_call" | custom-call | flops 1811939328 | bytes 8388608 | tf_op jit(solution)/shard_map/project_qkv/pallas_call | solution.py:103
  92.5 1.3 copy.46.scol_ref
  95.3 17.9 %attend.1 = (bf16[192,2048]{1,0:T(8,128)(2,1)}, f32[3,2048]{1,0:T(4,128)}) custom-call(s32[4]{0:T(128)} %get-tuple-element.127.lo_ref, s32[4]{0:T(128)} %get-tuple-element.126.hi_ref, bf16[192,2048]{1,0:T(8,128)(2,1)} %get-tuple-element.43.q_ref, bf16[192,2048]{1,0:T(8,128)(2,1)} %get-tuple-element.44.k_ref, bf16[192,2048]{1,0:T(8,128)(2,1)} %get-tuple-element.45.v_ref, ...), custom_call_target="tpu_custom_call" | custom-call | flops 6442450944 | bytes 8388608 | tf_op jit(solution)/shard_map/attend/pallas_call | solution.py:174
  113.2 66.6 %middle.1 = (f32[512,768]{1,0:T(8,128)}, f32[512,768]{1,0:T(8,128)}, bf16[192,2048]{1,0:T(8,128)(2,1)}, f32[8,24,640]{2,1,0:T(8,128)}, bf16[768,768]{1,0:T(8,128...) custom-call(bf16[192,2048]{1,0:T(8,128)(2,1)} %get-tuple-element.46., ...), custom_call_target="tpu_custom_call" | custom-call | flops 14495514624 | bytes 67108864 | tf_op jit(solution)/shard_map/middle/pallas_call | solution.py:1008
  179.8 1.2 collective-permute-start.3
  181.0 3.2 %collective-permute-start.1 = (bf16[2,4,96,768]{3,2,1,0:T(8,128)(2,1)}, bf16[2,4,96,768]{3,2,1,0:T(8,128)(2,1)S(1)}, u32[]{:S(2)}, u32[]{:S(2)}) collective-permute-start(bf16[2,4,96,768]{3,2,1,0:T(8,128)(2,1)} %get-tuple-element.55), channel_id=1, source_target_pairs={{0,4},{4,0},{8,12},{12,8},{16,20},{20,16},{24,28},{28,24},{1,5},{5... | collective-permute-start | bytes 3538952 | tf_op jit(solution)/shard_map/ppermute | solution.py:1164
  184.2 1.7 collective-permute-start.2
  185.9 26.4 %attend_back.1.refs_0_ = bf16[576,2048]{1,0:T(8,128)(2,1)} custom-call(s32[4]{0:T(128)} %get-tuple-element.127.lo_ref, s32[4]{0:T(128)} %get-tuple-element.126.hi_ref, bf16[192,2048]{1,0:T(8,128)(2,1)} %get-tuple-element.43.q_ref, bf16[192,2048]{1,0:T(8,128)(2,1)} %get-tuple-element.44.k_ref, bf16[192,2048]{1,0:T(8,128)(2,1)} %get-tuple-element.45.v_ref, ...), custom_call_target="tpu_custom_call" | custom-call | flops 16106127360 | bytes 8388608 | tf_op jit(solution)/shard_map/attend_back/pallas_call | solution.py:298
  212.4 4.5 %collective-permute-done.2 = bf16[768,768]{1,0:T(8,128)(2,1)S(1)} collective-permute-done((bf16[768,768]{1,0:T(8,128)(2,1)}, bf16[768,768]{1,0:T(8,128)(2,1)S(1)}, u32[]{:S(2)}, u32[]{:S(2)}) %collective-permute-start.2) | collective-permute-done | bytes 1179680 | tf_op jit(solution)/shard_map/ppermute | solution.py:1064
  216.9 1.0 copy-done.3
  217.9 65.7 %closing.1 = (f32[512,768]{1,0:T(8,128)}, f32[1,1536]{1,0:T(1,128)}, f32[8,24,2560]{2,1,0:T(8,128)}, f32[96,768]{1,0:T(8,128)}, f32[96,768]{1,0:T(8,128)}, /*index=5*/f32[96,192]{1,0:T(8,128)}, f32[96,576]{1,0:T(8,128)}) custom-call(bf16[576,2048]{1,0:T(8,128)(2,1)} %attend_back.1.refs_0_, bf16[2048,768]{1,0:T(8,128)(2,1)} %get-tuple-element.41.n_ref.refs_1_, ...), custom_call_target="tpu_custom_call" | custom-call | bytes 67108864 | tf_op jit(solution)/shard_map/closing/pallas_call | solution.py:684
  283.6 1.9 slice_reduce_fusion
  285.5 1.2 slice_reduce_fusion.1
  286.7 3.6 %convolution_bitcast_fusion = f32[128,2304]{1,0:T(8,128)} fusion(f32[8,24,2560]{2,1,0:T(8,128)} %get-tuple-element.66), kind=kOutput, calls=%fused_computation | convolution fusion | flops 452984832 | bytes 2424832 | tf_op jit(solution)/shard_map/dot_general | solution.py:1182
  292.2 0.7 copy.50
  293.1 0.9 copy.49
  293.9 1.1 copy.55
  295.1 0.8 copy-done.1
  295.9 1.1 copy.56
  297.1 0.7 copy.57
  (68 shorter events, 8.2 us)
Async XLA Ops:
  0.6 10.1 %copy-start.15 = (s32[1,16]{1,0:T(1,128)S(1)}, s32[1,16]{1,0:T(1,128)}, u32[]{:S(2)}) copy-start(s32[1,16]{1,0:T(1,128)} %param.17) | copy-start | bytes 196
  0.7 9.4 %copy-start.6 = (f32[768,96]{0,1:T(8,128)S(1)}, f32[768,96]{0,1:T(8,128)}, u32[]{:S(2)}) copy-start(f32[768,96]{0,1:T(8,128)} %param.26) | copy-start | bytes 884740
  0.7 11.3 %copy-start.13 = (f32[2304]{0:T(1024)S(1)}, f32[2304]{0:T(1024)}, u32[]{:S(2)}) copy-start(f32[2304]{0:T(1024)} %param.29) | copy-start | bytes 27652
  0.7 11.3 %copy-start.4 = (f32[128,2304]{1,0:T(8,128)S(1)}, f32[128,2304]{1,0:T(8,128)}, u32[]{:S(2)}) copy-start(f32[128,2304]{1,0:T(8,128)} %param.28) | copy-start | bytes 3538948
  10.9 81.6 %copy-start.11 = (s32[2048]{0:T(1024)}, s32[2048]{0:T(1024)S(1)}, u32[]{:S(2)}) copy-start(s32[2048]{0:T(1024)S(1)} %get-tuple-element.113) | copy-start | bytes 24580
  13.3 68.8 %copy-start.12 = (f32[3072]{0:T(1024)S(1)}, f32[3072]{0:T(1024)}, u32[]{:S(2)}) copy-start(f32[3072]{0:T(1024)} %param.25) | copy-start | bytes 36868
  82.0 31.2 %collective-permute-start = (bf16[768,768]{1,0:T(8,128)(2,1)}, bf16[768,768]{1,0:T(8,128)(2,1)}, u32[]{:S(2)}, u32[]{:S(2)}) collective-permute-start(bf16[768,768]{1,0:T(8,128)(2,1)} %bitcast.49), channel_id=1, source_target_pairs={{0,2},{1,3},{2,0},{3,1},{4,6},{5,7},{6,4},{7,5},{8,10},{9,11},{10,... | collective-permute-start | bytes 3538952 | tf_op jit(solution)/shard_map/ppermute | solution.py:1064
  85.3 6.0 %copy-start.16 = (f32[768]{0:T(1024)S(1)}, f32[768]{0:T(1024)}, u32[]{:S(2)}) copy-start(f32[768]{0:T(1024)} %param.23) | copy-start | bytes 9220
  85.3 6.6 %copy-start.17 = (f32[768]{0:T(1024)S(1)}, f32[768]{0:T(1024)}, u32[]{:S(2)}) copy-start(f32[768]{0:T(1024)} %param.27) | copy-start | bytes 9220
  179.8 32.5 %collective-permute-start.3 = (bf16[768,192]{1,0:T(8,128)(2,1)}, bf16[768,192]{1,0:T(8,128)(2,1)S(1)}, u32[]{:S(2)}, u32[]{:S(2)}) collective-permute-start(bf16[768,192]{1,0:T(8,128)(2,1)} %get-tuple-element.59), channel_id=1, source_target_pairs={{0,2},{1,3},{2,0},{3,1},{4,6},{5,7},{6,4},{7,5},{8,10},{9,11},{10,... | collective-permute-start | bytes 884744 | tf_op jit(solution)/shard_map/ppermute | solution.py:1064
  181.0 31.3 %collective-permute-start.1 = (bf16[2,4,96,768]{3,2,1,0:T(8,128)(2,1)}, bf16[2,4,96,768]{3,2,1,0:T(8,128)(2,1)S(1)}, u32[]{:S(2)}, u32[]{:S(2)}) collective-permute-start(bf16[2,4,96,768]{3,2,1,0:T(8,128)(2,1)} %get-tuple-element.55), channel_id=1, source_target_pairs={{0,4},{4,0},{8,12},{12,8},{16,20},{20,16},{24,28},{28,24},{1,5},{5... | collective-permute-start | bytes 3538952 | tf_op jit(solution)/shard_map/ppermute | solution.py:1164
  184.2 32.7 %collective-permute-start.2 = (bf16[768,768]{1,0:T(8,128)(2,1)}, bf16[768,768]{1,0:T(8,128)(2,1)S(1)}, u32[]{:S(2)}, u32[]{:S(2)}) collective-permute-start(bf16[768,768]{1,0:T(8,128)(2,1)} %get-tuple-element.57), channel_id=1, source_target_pairs={{0,2},{1,3},{2,0},{3,1},{4,6},{5,7},{6,4},{7,5},{8,10},{9,11},{10,... | collective-permute-start | bytes 3538952 | tf_op jit(solution)/shard_map/ppermute | solution.py:1064
  212.3 4.6 %copy-start.5 = (bf16[768,192]{1,0:T(8,128)(2,1)}, bf16[768,192]{1,0:T(8,128)(2,1)S(1)}, u32[]{:S(2)}) copy-start(bf16[768,192]{1,0:T(8,128)(2,1)S(1)} %collective-permute-done.3) | copy-start | bytes 884740
  212.4 4.6 %copy-start.2 = (bf16[2,4,96,768]{3,2,1,0:T(8,128)(2,1)}, bf16[2,4,96,768]{3,2,1,0:T(8,128)(2,1)S(1)}, u32[]{:S(2)}) copy-start(bf16[2,4,96,768]{3,2,1,0:T(8,128)(2,1)S(1)} %collective-permute-done.1.refs_4_) | copy-start | bytes 3538948
  216.9 1.0 copy-start.3
  285.5 5.4 %copy-start.14 = (f32[1,1536]{1,0:T(1,128)S(1)}, f32[1,1536]{1,0:T(1,128)}, u32[]{:S(2)}) copy-start(f32[1,1536]{1,0:T(1,128)} %get-tuple-element.63) | copy-start | bytes 18436
  285.5 6.6 %copy-start.10 = (f32[96,192]{1,0:T(8,128)S(1)}, f32[96,192]{1,0:T(8,128)}, u32[]{:S(2)}) copy-start(f32[96,192]{1,0:T(8,128)} %get-tuple-element.65) | copy-start | bytes 221188
  285.5 7.4 %copy-start.9 = (f32[96,576]{1,0:T(8,128)S(1)}, f32[96,576]{1,0:T(8,128)}, u32[]{:S(2)}) copy-start(f32[96,576]{1,0:T(8,128)} %get-tuple-element.64) | copy-start | bytes 663556
  286.7 7.2 %copy-start = (f32[512,768]{1,0:T(8,128)S(1)}, f32[512,768]{1,0:T(8,128)}, u32[]{:S(2)}) copy-start(f32[512,768]{1,0:T(8,128)} %get-tuple-element.141) | copy-start | bytes 4718596
  293.9 2.0 copy-start.1
  295.9 1.1 copy-start.8
  295.9 1.9 copy-start.7

commit v2 on v1

--- a/solution.py
+++ b/solution.py
@@ -377,11 +377,19 @@
 
 
 def opening_kernel(n_z, count, *refs):
-    x_ref, gain_ref, bias_ref, sel_ref, table_ref = refs[:5]
-    w_refs = refs[5 : 5 + count]
-    n_out, mod_out, w_outs = refs[5 + count], refs[6 + count], refs[7 + count : 7 + 2 * count]
-    n_ref, mod_s, local_sem, send_sem, recv_sem = refs[7 + 2 * count :]
+    x_ref, gain_ref, bias_ref, sel_ref, table_ref, qkv_ref, proj_ref, up_ref, down_ref = refs[:9]
+    n_out, mod_out, w_outs = refs[9], refs[10], refs[11 : 11 + count]
+    w_refs = refs[11 + count : 11 + 2 * count]
+    n_ref, mod_s, local_sem, send_sem, recv_sem = refs[11 + 2 * count :]
     links = Links(send_sem, recv_sem, n_z)
+    head_width = qkv_ref.shape[2]
+    for part in range(3):
+        w_refs[0][:, part * head_width : (part + 1) * head_width] = qkv_ref[part].astype(BF)
+    w_refs[1][...] = proj_ref[...].T.astype(BF)
+    half = w_refs[2].shape[1]
+    w_refs[2][...] = up_ref[:, :half].astype(BF)
+    w_refs[3][...] = down_ref[...].astype(BF)
+    w_refs[4][...] = up_ref[:, half:].astype(BF)
     greet([links.core, links.across, links.beside] + [links.along(k) for k in range(1, n_z)])
     rows = x_ref.shape[0]
 
@@ -399,7 +407,7 @@
     def norm_step(i, carry):
         here = pl.ds(pl.multiple_of(i * ROWS, ROWS), ROWS)
         normed, _ = normalize(x_ref[here, :])
-        n_ref[here, :] = (normed * gain_ref[...] + bias_ref[...]).astype(BF)
+        n_ref[here, :] = (normed * gain_ref[...][None, :] + bias_ref[...][None, :]).astype(BF)
         return carry
 
     def mod_step(i):
@@ -478,22 +486,27 @@
 def opening(x, gain, bias, sel, table, weights, n_dp, n_tensor):
     rows, width = x.shape
     n_z = n_dp // 2
-    count = len(weights)
+    qkv, proj, up, down = weights
+    depth = up.shape[0]
+    early = up.shape[1] * 2 // 3 // 128 * 128
+    columns = (3 * qkv.shape[2], proj.shape[0], early, down.shape[1], up.shape[1] - early)
+    count = len(columns)
     slots = count * (2 * n_z - 1) + 6 + n_dp
-    shapes = [(n_dp,) + w.shape for w in weights]
+    shapes = [(n_dp, depth, c) for c in columns]
     shapes[1] = (n_tensor,) + shapes[1]
     shapes[2] = (2,) + shapes[2]
     return pl.pallas_call(
         functools.partial(opening_kernel, n_z, count),
         name="opening",
-        in_specs=[pl.BlockSpec(memory_space=pltpu.VMEM)] * (5 + count),
+        in_specs=[pl.BlockSpec(memory_space=pltpu.VMEM)] * 9,
         out_specs=[pl.BlockSpec(memory_space=pl.ANY)] * (2 + count),
         out_shape=[
             jax.ShapeDtypeStruct((n_tensor * rows, width), BF),
             jax.ShapeDtypeStruct((rows, table.shape[1]), F32),
         ]
         + [jax.ShapeDtypeStruct(shape, BF) for shape in shapes],
-        scratch_shapes=[
+        scratch_shapes=[pltpu.VMEM((depth, c), BF) for c in columns]
+        + [
             pltpu.VMEM((rows, width), BF),
             pltpu.VMEM((rows, table.shape[1]), F32),
             pltpu.SemaphoreType.DMA((1 + count + rows // ROWS,)),
@@ -504,18 +517,19 @@
             collective_id=0, has_side_effects=True, vmem_limit_bytes=VMEM_LIMIT
         ),
         cost_estimate=pl.CostEstimate(flops=0, bytes_accessed=64 << 20, transcendentals=0),
-    )(x, gain[None, :], bias[None, :], sel, table, *weights)
-
-
-def closing_kernel(n_z, *refs):
+    )(x, gain, bias, sel, table, *weights)
+
+
+def closing_kernel(n_z, slot_count, embed_width, *refs):
     g_ref, n_ref, w_ref, up_keep, up_got, down_near, down_far, proj_near, proj_far = refs[:9]
     x_ref, h_ref, gain_ref, sums_ref = refs[9:13]
-    in_grad_ref, tail_ref, all_ref, up_out, down_out, proj_out, qkv_out = refs[13:20]
-    part_send, core_buf, y_send, y_recv, vec, all_vec, qkv_flat, qkv_ref = refs[20:28]
-    up_y_send, up_y_recv = refs[28:30]
-    x_send, x_recv = refs[30:32], refs[32:35]
-    z_send, z_recv = refs[35:39], refs[39:43]
-    send_sem, recv_sem = refs[43:]
+    in_grad_ref, tail_ref, time_ref, time_bias_ref, biases_ref = refs[13:18]
+    up_out, down_out, proj_out, qkv_out = refs[18:22]
+    all_ref, part_send, core_buf, y_send, y_recv, vec, all_vec, qkv_flat, qkv_ref = refs[22:31]
+    up_y_send, up_y_recv = refs[31:33]
+    x_send, x_recv = refs[33:35], refs[35:38]
+    z_send, z_recv = refs[38:42], refs[42:46]
+    send_sem, recv_sem = refs[46:]
     links = Links(send_sem, recv_sem, n_z)
     z, x = links.z, links.x
     n_dp = 2 * n_z
@@ -609,12 +623,6 @@
         return carry
 
     y_copy = links.send(y_send, y_recv, links.across)
-    here = all_ref.at[:, :, own_lanes]
-    there = all_ref.at[:, :, lanes(links.y_rank)]
-    sums_last = [
-        links.send(sums_ref, here, links.across),
-        links.send(sums_ref, here, links.core),
-    ]
     lax.fori_loop(0, width // strip, qkv_step, 0)
     depth = qkv_ref.shape[2]
     for r in range(n_dp):
@@ -633,10 +641,16 @@
         [jnp.sum(grad * normed, axis=0, keepdims=True), jnp.sum(grad, axis=0, keepdims=True)], axis=1
     )
     vec[links.t] = own_vec
-    in_grad_ref[...] = h_ref[...] + norm_back(grad * gain_ref[...], normed, inverse)
+    in_grad_ref[...] = h_ref[...] + norm_back(grad * gain_ref[...][None, :], normed, inverse)
     tensor_sends = [
         links.send(vec.at[links.t], vec.at[links.t], peer)
         for peer in (links.core, links.across, diagonal)
+    ]
+    here = all_ref.at[:, :, own_lanes]
+    there = all_ref.at[:, :, lanes(links.y_rank)]
+    sums_last = [
+        links.send(sums_ref, here, links.across),
+        links.send(sums_ref, here, links.core),
     ]
     finish(1)
     for copy in tensor_sends:
@@ -648,14 +662,27 @@
     sums_last.append(links.send(there, there, links.core))
     finish(2)
     finish(3)
+    sums_last[1].wait_recv()
+    sums_last[2].wait_recv()
+    mod_width = 3 * width
+    mods = jnp.concatenate([all_ref[r, :slot_count, :mod_width] for r in range(n_dp)], axis=0)
+    embeds = jnp.concatenate(
+        [all_ref[r, :slot_count, mod_width : mod_width + embed_width] for r in range(n_dp)], axis=0
+    )
+    time_ref[...] = lax.dot_general(
+        embeds, mods, (((0,), (0,)), ((), ())), precision=highest, preferred_element_type=F32
+    )
+    time_bias_ref[...] = jnp.sum(mods, axis=0, keepdims=True)
+    biases = all_ref[0, slot_count:, : 2 * width]
+    for r in range(1, n_dp):
+        biases = biases + all_ref[r, slot_count:, : 2 * width]
+    biases_ref[...] = biases
     for copy in dp_sends:
         copy.wait_recv()
     total = all_vec[0]
     for r in range(1, n_dp):
         total = total + all_vec[r]
     tail_ref[...] = total
-    sums_last[1].wait_recv()
-    sums_last[2].wait_recv()
     for copy in [c1, c3, y_copy] + dp_sends + sums_last + tensor_sends:
         copy.wait_send()
     for s in range(n_z):
@@ -667,7 +694,9 @@
                 z_copy(n, s).wait_send()
 
 
-def closing(qkv_grad, normed, weight, up, down, proj, residual_in, hidden_grad, gain, sums, n_dp):
+def closing(
+    qkv_grad, normed, weight, up, down, proj, residual_in, hidden_grad, gain, sums, n_dp, slot_count, embed_width
+):
     rows, width = residual_in.shape
     head_width = weight.shape[1]
     n_z = n_dp // 2
@@ -682,17 +711,20 @@
     slots = 8 * n_z + 2 + 1 + 3 + 3 + (n_dp - 1)
     vmem = pl.BlockSpec(memory_space=pltpu.VMEM)
     out = pl.pallas_call(
-        functools.partial(closing_kernel, n_z),
+        functools.partial(closing_kernel, n_z, slot_count, embed_width),
         name="closing",
         in_specs=[vmem] * 13,
-        out_specs=[vmem] * 7,
+        out_specs=[vmem] * 9,
         out_shape=[
             jax.ShapeDtypeStruct((rows, width), F32),
             jax.ShapeDtypeStruct((1, 2 * width), F32),
-            jax.ShapeDtypeStruct(sums.shape[:2] + (4 * sums.shape[2],), F32),
+            jax.ShapeDtypeStruct((embed_width, 3 * width), F32),
+            jax.ShapeDtypeStruct((1, 3 * width), F32),
+            jax.ShapeDtypeStruct((sums.shape[1] - slot_count, 2 * width), F32),
         ]
         + [jax.ShapeDtypeStruct(shape, F32) for shape in shards],
         scratch_shapes=[
+            pltpu.VMEM(sums.shape[:2] + (4 * sums.shape[2],), F32),
             pltpu.VMEM((2, rows, width), BF),
             pltpu.VMEM((2, rows, width), BF),
             pltpu.VMEM((rows, width), BF),
@@ -721,10 +753,10 @@
         *blocks(proj),
         residual_in,
         hidden_grad,
-        gain[None, :],
+        gain,
         sums,
     )
-    return out[0], out[1].reshape(2, width), out[2], out[3:]
+    return out[0], out[1], out[2:5], out[5:]
 
 
 def middle_kernel(n_z, *refs):
@@ -732,6 +764,8 @@
         mixed_ref,
         proj_ref,
         up_hbm,
+        up_late_hbm,
+        up_late_far_hbm,
         down_hbm,
         down_far_hbm,
         x_ref,
@@ -742,9 +776,9 @@
         proj_bias_ref,
         up_bias_ref,
         down_bias_ref,
-    ) = refs[:13]
-    out_ref, h_grad_ref, mixed_grad_ref, packs_ref, down_near, proj_near, down_far, proj_far = refs[13:21]
-    up_keep, up_away = refs[21:23]
+    ) = refs[:15]
+    out_ref, h_grad_ref, mixed_grad_ref, packs_ref, down_near, proj_near, down_far, proj_far = refs[15:23]
+    up_keep, up_away = refs[23:25]
     (
         mix_buf,
         mix_t,
@@ -769,10 +803,11 @@
         proj_recv,
         sums_ref,
         sums_buf,
+        early_s,
         local_sem,
         send_sem,
         recv_sem,
-    ) = refs[23:]
+    ) = refs[25:]
     links = Links(send_sem, recv_sem, n_z)
     depth = up_keep.shape[2]
     rows, width = x_ref.shape
@@ -789,17 +824,21 @@
     mix_copies = [
         links.send(mixed_ref.at[:, lanes(ranks[d])], mix_buf.at[d], peers[d]) for d in (3, 2, 1)
     ]
-    w_copies = [
-        links.send(up_hbm.at[0], up_buf.at[1], links.core),
-        links.send(down_hbm, down_buf.at[1], links.core),
-        links.send(up_hbm.at[1], up_buf.at[3], links.core),
-        links.send(down_far_hbm, down_buf.at[3], links.core),
-    ]
+    half = up_hbm.shape[2]
+
+    def pieces(shift):
+        return [
+            (up_hbm.at[0], up_buf.at[shift, :, :half]),
+            (up_late_hbm, up_buf.at[shift, :, half:]),
+            (down_hbm, down_buf.at[shift]),
+            (up_hbm.at[1], up_buf.at[2 + shift, :, :half]),
+            (up_late_far_hbm, up_buf.at[2 + shift, :, half:]),
+            (down_far_hbm, down_buf.at[2 + shift]),
+        ]
+
+    w_copies = [links.send(src, dst, links.core) for src, dst in pieces(1)]
     local = [
-        pltpu.make_async_copy(up_hbm.at[0], up_buf.at[0], local_sem.at[0]),
-        pltpu.make_async_copy(down_hbm, down_buf.at[0], local_sem.at[1]),
-        pltpu.make_async_copy(up_hbm.at[1], up_buf.at[2], local_sem.at[2]),
-        pltpu.make_async_copy(down_far_hbm, down_buf.at[2], local_sem.at[3]),
+        pltpu.make_async_copy(src, dst, local_sem.at[i]) for i, (src, dst) in enumerate(pieces(0))
     ]
     for copy in local:
         copy.start()
@@ -819,6 +858,15 @@
     down_bias_sum = tiles(gate_step, jnp.zeros((1, width), F32))
     dz_t[...] = dz_s[...].T
     sums_ref[...] = jnp.zeros_like(sums_ref)
+    for e, copy in ((0, local[2]), (1, local[5])):
+        copy.wait()
+
+        def early_step(i, carry):
+            here = pl.ds(pl.multiple_of(i * STRIP, STRIP), STRIP)
+            early_s[e, here, :] = dot(dz_s[here, :], down_buf[2 * e], 1, 0)
+            return carry
+
+        lax.fori_loop(0, rows // STRIP, early_step, 0)
     mix_t[0] = mixed_ref[:, lanes(links.t)].T
     for d, copy in zip((3, 2, 1), mix_copies):
         copy.wait_recv()
@@ -826,7 +874,7 @@
 
     def hidden_step(i, carry):
         here = tile(i)
-        hidden = x_ref[here, :] + proj_bias_ref[...]
+        hidden = x_ref[here, :] + proj_bias_ref[...][None, :]
         for d in range(4):
             hidden = hidden + dot(mix_t[d, here, :], proj_ref[d], 1, 1)
         hid_s[here, :] = hidden
@@ -842,7 +890,7 @@
     m_acc[...] = jnp.zeros_like(m_acc)
     root = math.sqrt(2.0 / math.pi)
 
-    def feed(d):
+    def feed(d, early=None):
         up = up_buf.at[d]
         down = down_buf.at[d]
 
@@ -855,7 +903,8 @@
             act = (u * half).astype(BF)
             act_s[here, :] = act
             slope = half + 0.5 * u * (1.0 - bend * bend) * (root * (1.0 + 3.0 * 0.044715 * square))
-            du = dot(dz_s[here, :], down[...], 1, 0) * slope
+            act_grad = dot(dz_s[here, :], down[...], 1, 0) if early is None else early[here, :]
+            du = act_grad * slope
             low = du.astype(BF)
             du_s[here, :] = low
             z_acc[here, :] += dot(act, down[...], 1, 1)
@@ -901,11 +950,11 @@
     for e in range(2):
         up_copy(e).start()
         down_copy(e).start()
-    for copy in local:
-        copy.wait()
+    for i in (0, 1, 3, 4):
+        local[i].wait()
 
     for e, down_sum in ((1, down_far), (0, down_near)):
-        feed(2 * e)
+        feed(2 * e, early_s.at[e])
         up_copy(e).wait_recv()
         down_copy(e).wait_recv()
 
@@ -933,7 +982,7 @@
         scale = mod_ref[here, :width]
         gate = mod_ref[here, 2 * width :]
         grad = grad_ref[here, :]
-        branch = z_acc[here, :] + down_bias_ref[...]
+        branch = z_acc[here, :] + down_bias_ref[...][None, :]
         shift_grad = m_acc[here, :]
         out_ref[here, :] = hidden + gate * branch
         h_grad = grad + norm_back(shift_grad * (1.0 + scale), normed, inverse)
@@ -994,21 +1043,21 @@
 
 
 def middle(
-    mixed, proj, up, down, down_far, x, grad, mod, sel, embed, proj_bias, up_bias, down_bias, n_dp
+    mixed, proj, weights, x, grad, mod, sel, embed, proj_bias, up_bias, down_bias, n_dp
 ):
     rows, width = x.shape
     head_width, total_rows = mixed.shape
-    units = down.shape[1]
+    units = weights[3].shape[1]
     vmem = pl.BlockSpec(memory_space=pltpu.VMEM)
     hbm = pl.BlockSpec(memory_space=pl.ANY)
     sums = (sel.shape[0], -(-(3 * width + embed.shape[1]) // 512) * 512)
-    slots = 3 + 4 + 4 + 3 + 2 + 3 + (n_dp - 1)
+    slots = 3 + 6 + 4 + 3 + 2 + 3 + (n_dp - 1)
     square = (2, width, units)
     halves = (2, n_dp // 2, width // n_dp, units)
     return pl.pallas_call(
         functools.partial(middle_kernel, n_dp // 2),
         name="middle",
-        in_specs=[vmem, vmem, hbm, hbm, hbm] + [vmem] * 8,
+        in_specs=[vmem, vmem] + [hbm] * 5 + [vmem] * 8,
         out_specs=[vmem] * 10,
         out_shape=[
             jax.ShapeDtypeStruct((rows, width), F32),
@@ -1046,7 +1095,8 @@
             pltpu.VMEM((2, width, head_width), BF),
             pltpu.VMEM(sums, F32),
             pltpu.VMEM((4, sums[0], sums[1] // 4), F32),
-            pltpu.SemaphoreType.DMA((4,)),
+            pltpu.VMEM((2, rows, units), F32),
+            pltpu.SemaphoreType.DMA((6,)),
             pltpu.SemaphoreType.DMA((slots,)),
             pltpu.SemaphoreType.DMA((slots,)),
         ],
@@ -1056,7 +1106,75 @@
         cost_estimate=pl.CostEstimate(
             flops=12 * rows * width * units * 4, bytes_accessed=64 << 20, transcendentals=0
         ),
-    )(mixed, proj, up, down, down_far, x, grad, mod, sel, embed, proj_bias, up_bias, down_bias)
+    )(mixed, proj, *weights, x, grad, mod, sel, embed, proj_bias, up_bias, down_bias)
+
+
+def results_kernel(*refs):
+    out_ref, in_grad_ref, tail_ref, time_ref, time_bias_ref, biases_ref = refs[:6]
+    up_ref, down_ref, proj_ref, qkv_ref = refs[6:10]
+    (
+        out,
+        in_grad,
+        gain,
+        bias,
+        qkv,
+        proj,
+        proj_bias,
+        up,
+        up_bias,
+        down,
+        down_bias,
+        time,
+        time_bias,
+    ) = refs[10:]
+    width = out.shape[1]
+    out[...] = out_ref[...]
+    in_grad[...] = in_grad_ref[...]
+    gain[...] = tail_ref[0, :width]
+    bias[...] = tail_ref[0, width:]
+    columns = qkv.shape[2]
+    for part in range(3):
+        qkv[part] = qkv_ref[:, part * columns : (part + 1) * columns]
+    proj[...] = proj_ref[...].T
+    down[...] = down_ref[...]
+    up[...] = up_ref[...]
+    proj_bias[...] = biases_ref[0, :width]
+    down_bias[...] = biases_ref[0, width:]
+    units = up.shape[1]
+    for r in range(up_bias.shape[0] // units):
+        up_bias[r * units : (r + 1) * units] = biases_ref[1 + r, :units]
+    time[...] = time_ref[...]
+    time_bias[...] = time_bias_ref[0, :]
+
+
+def results(residual_out, in_grad, tail, times, grads, tensor_units):
+    rows, width = in_grad.shape
+    depth, units = grads[0].shape
+    columns = grads[2].shape[1]
+    shapes = [
+        (rows, width),
+        (rows, width),
+        (width,),
+        (width,),
+        (3, depth, columns),
+        (columns, depth),
+        (width,),
+        (depth, units),
+        (tensor_units,),
+        (depth, units),
+        (width,),
+        times[0].shape,
+        (times[0].shape[1],),
+    ]
+    vmem = pl.BlockSpec(memory_space=pltpu.VMEM)
+    return pl.pallas_call(
+        results_kernel,
+        name="results",
+        in_specs=[vmem] * 10,
+        out_specs=[vmem] * len(shapes),
+        out_shape=[jax.ShapeDtypeStruct(shape, F32) for shape in shapes],
+        compiler_params=pltpu.CompilerParams(vmem_limit_bytes=VMEM_LIMIT),
+    )(residual_out, in_grad, tail, *times, *grads)
 
 
 def to_tensor_peer(value, distance):
@@ -1107,26 +1225,22 @@
     up_bias_rel = jnp.stack(
         [lax.dynamic_slice_in_dim(up_bias, ranks[d] * units, units)[None] for d in range(n_tensor)]
     )
-    qkv_shard = jnp.transpose(qkv_weight, (1, 0, 2)).reshape(qkv_weight.shape[1], -1).astype(BF)
-    normed_full, modulation, qkv_full, proj_all, up_own, down_own = opening(
+    normed_full, modulation, qkv_full, proj_all, up_both, down_own, up_late = opening(
         residual_in,
         norm_gain,
         norm_bias,
         onehot,
         mod_table,
-        (
-            qkv_shard,
-            proj_weight.T.astype(BF),
-            up_weight.astype(BF),
-            down_weight.T.astype(BF),
-        ),
+        (qkv_weight, proj_weight, up_weight, down_weight.T),
         n_dp,
         n_tensor,
     )
     qkv_full = qkv_full.reshape(width_model, -1)
     proj_all = proj_all.reshape(n_tensor, width_model, -1)
-    up_both = up_own.reshape(2, width_model, -1)
+    up_both = up_both.reshape(2, width_model, -1)
     down_own = down_own.reshape(width_model, -1)
+    up_late = up_late.reshape(width_model, -1)
+    up_late_far = to_tensor_peer(up_late, 2)
     down_far = to_tensor_peer(down_own, 2)
 
     cos, sin = rope_tables(positions)
@@ -1139,17 +1253,15 @@
     outs = middle(
         mixed,
         proj_all,
-        up_both,
-        down_own,
-        down_far,
+        (up_both, up_late, up_late_far, down_own, down_far),
         residual_in,
         out_grad,
         modulation,
         chosen.astype(F32),
         own_embed,
-        proj_bias[None, :],
+        proj_bias,
         up_bias_rel,
-        down_bias[None, :],
+        down_bias,
         n_dp,
     )
     residual_out, hidden_grad, mixed_grad, sums, down_near, proj_near, down_other, proj_other = outs[:8]
@@ -1162,9 +1274,8 @@
     proj_far = to_tensor_peer(proj_other, 2)
     down_far = to_tensor_peer(down_other, 2)
     up_got = lax.ppermute(up_away, "dp", [(r, r ^ 1) for r in range(n_dp)])
-    embed_width, mod_width = time_weight.shape
-
-    input_grad, tail, packs, grads = closing(
+
+    input_grad, tail, times, grads = closing(
         qkv_grad,
         normed_full,
         qkv_full,
@@ -1176,36 +1287,12 @@
         norm_gain,
         sums,
         n_dp,
-    )
-    all_mod = packs[:, :slot_count, :mod_width].reshape(-1, mod_width)
-    all_embed = packs[:, :slot_count, mod_width : mod_width + embed_width].reshape(-1, embed_width)
-    grad_time_weight = lax.dot_general(
-        all_embed, all_mod, (((0,), (0,)), ((), ())), precision=highest
-    )
-    grad_time_bias = jnp.sum(all_mod, axis=0)
-    biases = jnp.sum(packs[:, slot_count : slot_count + 1 + n_tensor], axis=0)
-    grad_proj_bias = biases[0, :width_model]
-    grad_down_bias = biases[0, width_model : 2 * width_model]
-    grad_up_bias = biases[1:, :units].reshape(-1)
-    grad_up, grad_down, grad_proj, grad_qkv = grads
-    grad_down = grad_down.T
-    grad_proj = grad_proj.T
-    grad_qkv = grad_qkv.reshape(grad_qkv.shape[0], 3, head_width).transpose(1, 0, 2)
-    return (
-        residual_out,
-        input_grad,
-        tail[0],
-        tail[1],
-        grad_qkv,
-        grad_proj,
-        grad_proj_bias,
-        grad_up,
-        grad_up_bias,
-        grad_down,
-        grad_down_bias,
-        grad_time_weight,
-        grad_time_bias,
-    )
+        slot_count,
+        time_weight.shape[0],
+    )
+    done = list(results(residual_out, input_grad, tail, times, grads, up_bias.shape[0]))
+    done[9] = done[9].T
+    return tuple(done)
 
 
 def solution(mesh):

time: 299 us -> 277 us (0.926)
  local copies, waits for them, and re-layouts: 17.7 us -> 3.21 us
  other arithmetic: 13.1 us -> 7.1 us
  Pallas kernels: 251 us -> 247 us
  waiting for transfers between devices: 4.56 us -> 8.03 us
    pallas_call x1, Pallas kernels: 68.6 us -> 59 us  [opening(): pl.pallas_call(functools.partial(opening_kernel, n_z, count), name='openi...]
    unnamed x43 -> x14, local copies, waits for them, and re-layouts: 8.85 us -> 1.03 us
    pallas_call x1 -> x2, Pallas kernels: 65.7 us -> 70.9 us  [the longest x1 65.9 us: closing(): pl.pallas_call(functools.partial(closing_kernel, n_z, slot_count, embed_w...]
    broadcast_in_dim x4 -> x0, local copies, waits for them, and re-layouts: 3.69 us -> none  [the longest x1 1.27 us: opening(): gain[None, :]]
    dot_general x1 -> x0, matrix products: 3.58 us -> none  [shards(): lax.dot_general(all_embed, all_mod, (((0,), (0,)), ((), ())), precision=h...]
    ppermute x3 -> x4, waiting for transfers between devices: 4.56 us -> 8.03 us  [to_tensor_peer(): lax.ppermute(value, 'tensor', [(r, r ^ distance) for r in range(size)])]
    convert_element_type x3 -> x0, other arithmetic: 3.29 us -> none  [the longest x1 1.64 us: shards(): up_weight.astype(BF)]
    reduce_sum x2 -> x0, other arithmetic: 3.13 us -> none  [the longest x1 1.95 us: shards(): grad_time_bias = jnp.sum(all_mod, axis=0)]
  transfers between devices with their start and end apart: 4 -> 5, of which waited for: 1 -> 2; matrix products, arithmetic and copies ran while one was open for 2% -> 2% of each run, Pallas kernels for 17% -> 18%
where the time goes in v2:
time: 277 us; the launch traced here: 276 us
  Pallas kernels  247 us (89%)
  waiting for transfers between devices  8.03 us (3%)
  starting transfers between devices  7.35 us (3%)
  other arithmetic  7.1 us (3%)
  local copies, waits for them, and re-layouts  3.21 us (1%)
    pallas_call x1, Pallas kernels, middle(): pl.pallas_call(functools.partial(middle_kernel, n_dp // 2), name='middle'...  66.9 us
    pallas_call x1, Pallas kernels, closing(): pl.pallas_call(functools.partial(closing_kernel, n_z, slot_count, embed_w...  65.9 us
    pallas_call x1, Pallas kernels, opening(): pl.pallas_call(functools.partial(opening_kernel, n_z, count), name='openi...  59 us
    pallas_call x1, Pallas kernels, attend_back(): pl.pallas_call(functools.partial(attend_back_kernel, heads), name='attend...  26.5 us
    pallas_call x1, Pallas kernels, attend(): pl.pallas_call(functools.partial(attend_kernel, heads), name='attend', gr...  18 us
    ppermute x4, waiting for transfers between devices, to_tensor_peer(): lax.ppermute(value, 'tensor', [(r, r ^ distance) for r in range(size)])  8.03 us
    pallas_call x1, Pallas kernels, project(): pl.pallas_call(functools.partial(project_kernel, heads), name='project_qk...  5.96 us
  transfers between devices with their start and end apart: 5, of which 2 were waited for; matrix products, arithmetic and copies ran while one was open for 2% of the time, Pallas kernels for 18%

profile of v2, /device:TPU:0, one launch (start us, length us, event | category | flops | bytes accessed | tf_op | source)
XLA Modules:
  0.0 276.5 jit_solution(12433578278214189235)
XLA Ops:
  0.7 0.7 convert_bitcast_fusion
  1.3 0.7 copy.32
  2.1 0.1 reduce
  2.2 0.8 select_reduce_fusion
  3.0 0.1 broadcast_compare_fusion
  3.1 0.8 fusion.refs_3_
  3.9 0.1 multiply_cosine_fusion.1
  4.0 2.6 convolution_add_fusion.refs_4_
  6.7 59.0 %opening.1 = (bf16[2048,768]{1,0:T(8,128)(2,1)}, f32[512,2304]{1,0:T(8,128)}, bf16[8,96,576]{2,1,0:T(8,128)(2,1)}, bf16[4,8,96,192]{3,2,1,0:T(8,128)(2,1)}, bf16...) custom-call(f32[512,768]{1,0:T(8,128)} %refs_9_.1, f32[768]{0:T(1024)} %refs_11_.1, ...), custom_call_target="tpu_custom_call" | custom-call | bytes 67108864 | tf_op jit(solution)/shard_map/opening/pallas_call | solution.py:498
  65.7 0.2 collective-permute-start
  65.9 1.8 collective-permute-start.1
  67.8 0.2 select_reduce_fusion.1
  68.0 0.5 and_select_fusion
  68.5 1.8 multiply_sine_fusion
  70.3 6.0 %project_qkv.1 = (bf16[192,2048]{1,0:T(8,128)(2,1)}, bf16[192,2048]{1,0:T(8,128)(2,1)}, bf16[192,2048]{1,0:T(8,128)(2,1)}) custom-call(bf16[2048,768]{1,0:T(8,128)(2,1)} %get-tuple-element.57.n_ref.refs_1_, bf16[768,576]{1,0:T(8,128)(2,1)} %bitcast.20, f32[32,2048]{1,0:T(8,128)} %get-tuple-element.112.cos_ref, f32[32,2048]{1,0:T(8,128)} %get-tuple-element.111.sin_ref), custom_call_target="tpu_custom_call" | custom-call | flops 1811939328 | bytes 8388608 | tf_op jit(solution)/shard_map/project_qkv/pallas_call | solution.py:103
  76.3 1.3 copy.33.scol_ref
  77.6 0.1 fusion.4
  77.7 18.0 %attend.1 = (bf16[192,2048]{1,0:T(8,128)(2,1)}, f32[3,2048]{1,0:T(4,128)}) custom-call(s32[4]{0:T(128)} %get-tuple-element.116.lo_ref, s32[4]{0:T(128)} %get-tuple-element.115.hi_ref, bf16[192,2048]{1,0:T(8,128)(2,1)} %get-tuple-element.59.q_ref, bf16[192,2048]{1,0:T(8,128)(2,1)} %get-tuple-element.60.k_ref, bf16[192,2048]{1,0:T(8,128)(2,1)} %get-tuple-element.61.v_ref, ...), custom_call_target="tpu_custom_call" | custom-call | flops 6442450944 | bytes 8388608 | tf_op jit(solution)/shard_map/attend/pallas_call | solution.py:174
  95.7 0.7 broadcast_select_fusion.refs_11_
  96.4 0.6 pad_maximum_fusion.refs_13_
  97.0 0.6 fusion.2.refs_10_
  97.7 3.3 %collective-permute-done.1.refs_6_ = bf16[768,768]{1,0:T(8,128)(2,1)} collective-permute-done((bf16[768,768]{1,0:T(8,128)(2,1)}, bf16[768,768]{1,0:T(8,128)(2,1)}, u32[]{:S(2)}, u32[]{:S(2)}) %collective-permute-start.1) | collective-permute-done | bytes 1179680 | tf_op jit(solution)/shard_map/ppermute | solution.py:1182
  101.0 66.9 %middle.1 = (f32[512,768]{1,0:T(8,128)}, f32[512,768]{1,0:T(8,128)}, bf16[192,2048]{1,0:T(8,128)(2,1)}, f32[8,24,640]{2,1,0:T(8,128)}, bf16[768,768]{1,0:T(8,128...) custom-call(bf16[192,2048]{1,0:T(8,128)(2,1)} %get-tuple-element.62., ...), custom_call_target="tpu_custom_call" | custom-call | flops 14495514624 | bytes 67108864 | tf_op jit(solution)/shard_map/middle/pallas_call | solution.py:1057
  167.8 0.6 collective-permute-start.4
  168.4 3.9 %collective-permute-start.2 = (bf16[2,4,96,768]{3,2,1,0:T(8,128)(2,1)}, bf16[2,4,96,768]{3,2,1,0:T(8,128)(2,1)S(1)}, u32[]{:S(2)}, u32[]{:S(2)}) collective-permute-start(bf16[2,4,96,768]{3,2,1,0:T(8,128)(2,1)} %get-tuple-element.72), channel_id=1, source_target_pairs={{0,4},{4,0},{8,12},{12,8},{16,20},{20,16},{24,28},{28,24},{1,5},{5... | collective-permute-start | bytes 3538952 | tf_op jit(solution)/shard_map/ppermute | solution.py:1276
  172.4 0.7 collective-permute-start.3
  173.1 26.5 %attend_back.1.refs_0_ = bf16[576,2048]{1,0:T(8,128)(2,1)} custom-call(s32[4]{0:T(128)} %get-tuple-element.116.lo_ref, s32[4]{0:T(128)} %get-tuple-element.115.hi_ref, bf16[192,2048]{1,0:T(8,128)(2,1)} %get-tuple-element.59.q_ref, bf16[192,2048]{1,0:T(8,128)(2,1)} %get-tuple-element.60.k_ref, bf16[192,2048]{1,0:T(8,128)(2,1)} %get-tuple-element.61.v_ref, ...), custom_call_target="tpu_custom_call" | custom-call | flops 16106127360 | bytes 8388608 | tf_op jit(solution)/shard_map/attend_back/pallas_call | solution.py:298
  199.6 0.0 copy-start
  199.6 4.7 %collective-permute-done.3 = bf16[768,768]{1,0:T(8,128)(2,1)S(1)} collective-permute-done((bf16[768,768]{1,0:T(8,128)(2,1)}, bf16[768,768]{1,0:T(8,128)(2,1)S(1)}, u32[]{:S(2)}, u32[]{:S(2)}) %collective-permute-start.3) | collective-permute-done | bytes 1179680 | tf_op jit(solution)/shard_map/ppermute | solution.py:1182
  204.4 1.0 copy-done.1
  205.4 65.9 %closing.1 = (f32[512,768]{1,0:T(8,128)}, f32[1,1536]{1,0:T(1,128)}, f32[128,2304]{1,0:T(8,128)}, f32[1,2304]{1,0:T(1,128)}, f32[8,1536]{1,0:T(8,128)}, /*index=...) custom-call(bf16[576,2048]{1,0:T(8,128)(2,1)} %attend_back.1.refs_0_, ...), custom_call_target="tpu_custom_call" | custom-call | bytes 67108864 | tf_op jit(solution)/shard_map/closing/pallas_call | solution.py:713
  271.3 5.0 %results.1 = (f32[512,768]{1,0:T(8,128)}, f32[512,768]{1,0:T(8,128)}, f32[768]{0:T(1024)}, f32[768]{0:T(1024)}, f32[3,96,192]{2,1,0:T(8,128)}, /*index=5*/f32[19...) custom-call(f32[512,768]{1,0:T(8,128)} %get-tuple-element.68.refs_0_, ...), custom_call_target="tpu_custom_call" | custom-call | tf_op jit(solution)/shard_map/results/pallas_call | solution.py:1170
  (25 shorter events, 0.1 us)
Async XLA Ops:
  3.0 73.3 %copy-start.3 = (s32[2048]{0:T(1024)}, s32[2048]{0:T(1024)S(1)}, u32[]{:S(2)}) copy-start(s32[2048]{0:T(1024)S(1)} %get-tuple-element.102) | copy-start | bytes 24580
  6.6 61.1 %copy-start.5 = (s32[1,16]{1,0:T(1,128)S(1)}, s32[1,16]{1,0:T(1,128)}, u32[]{:S(2)}) copy-start(s32[1,16]{1,0:T(1,128)} %param.17) | copy-start | bytes 196
  65.7 32.0 %collective-permute-start = (bf16[768,256]{1,0:T(8,128)(2,1)}, bf16[768,256]{1,0:T(8,128)(2,1)S(1)}, u32[]{:S(2)}, u32[]{:S(2)}) collective-permute-start(bf16[768,256]{1,0:T(8,128)(2,1)} %bitcast.35), channel_id=1, source_target_pairs={{0,2},{1,3},{2,0},{3,1},{4,6},{5,7},{6,4},{7,5},{8,10},{9,11},{10,... | collective-permute-start | bytes 1179656 | tf_op jit(solution)/shard_map/ppermute | solution.py:1182
  65.9 35.1 %collective-permute-start.1 = (bf16[768,768]{1,0:T(8,128)(2,1)}, bf16[768,768]{1,0:T(8,128)(2,1)}, u32[]{:S(2)}, u32[]{:S(2)}) collective-permute-start(bf16[768,768]{1,0:T(8,128)(2,1)} %bitcast.33), channel_id=1, source_target_pairs={{0,2},{1,3},{2,0},{3,1},{4,6},{5,7},{6,4},{7,5},{8,10},{9,11},{10,... | collective-permute-start | bytes 3538952 | tf_op jit(solution)/shard_map/ppermute | solution.py:1182
  70.3 7.3 %copy-start.4 = (f32[3072]{0:T(1024)S(1)}, f32[3072]{0:T(1024)}, u32[]{:S(2)}) copy-start(f32[3072]{0:T(1024)} %param.25) | copy-start | bytes 36868
  97.7 3.3 %copy-start.6 = (bf16[768,256]{1,0:T(8,128)(2,1)}, bf16[768,256]{1,0:T(8,128)(2,1)S(1)}, u32[]{:S(2)}) copy-start(bf16[768,256]{1,0:T(8,128)(2,1)S(1)} %collective-permute-done.refs_4_) | copy-start | bytes 1179652
  167.8 31.8 %collective-permute-start.4 = (bf16[768,192]{1,0:T(8,128)(2,1)}, bf16[768,192]{1,0:T(8,128)(2,1)S(1)}, u32[]{:S(2)}, u32[]{:S(2)}) collective-permute-start(bf16[768,192]{1,0:T(8,128)(2,1)} %get-tuple-element.76), channel_id=1, source_target_pairs={{0,2},{1,3},{2,0},{3,1},{4,6},{5,7},{6,4},{7,5},{8,10},{9,11},{10,... | collective-permute-start | bytes 884744 | tf_op jit(solution)/shard_map/ppermute | solution.py:1182
  168.4 31.2 %collective-permute-start.2 = (bf16[2,4,96,768]{3,2,1,0:T(8,128)(2,1)}, bf16[2,4,96,768]{3,2,1,0:T(8,128)(2,1)S(1)}, u32[]{:S(2)}, u32[]{:S(2)}) collective-permute-start(bf16[2,4,96,768]{3,2,1,0:T(8,128)(2,1)} %get-tuple-element.72), channel_id=1, source_target_pairs={{0,4},{4,0},{8,12},{12,8},{16,20},{20,16},{24,28},{28,24},{1,5},{5... | collective-permute-start | bytes 3538952 | tf_op jit(solution)/shard_map/ppermute | solution.py:1276
  172.4 32.0 %collective-permute-start.3 = (bf16[768,768]{1,0:T(8,128)(2,1)}, bf16[768,768]{1,0:T(8,128)(2,1)S(1)}, u32[]{:S(2)}, u32[]{:S(2)}) collective-permute-start(bf16[768,768]{1,0:T(8,128)(2,1)} %get-tuple-element.74), channel_id=1, source_target_pairs={{0,2},{1,3},{2,0},{3,1},{4,6},{5,7},{6,4},{7,5},{8,10},{9,11},{10,... | collective-permute-start | bytes 3538952 | tf_op jit(solution)/shard_map/ppermute | solution.py:1182
  199.6 4.8 %copy-start.2 = (bf16[768,192]{1,0:T(8,128)(2,1)}, bf16[768,192]{1,0:T(8,128)(2,1)S(1)}, u32[]{:S(2)}) copy-start(bf16[768,192]{1,0:T(8,128)(2,1)S(1)} %collective-permute-done.4) | copy-start | bytes 884740
  199.6 4.7 %copy-start = (bf16[2,4,96,768]{3,2,1,0:T(8,128)(2,1)}, bf16[2,4,96,768]{3,2,1,0:T(8,128)(2,1)S(1)}, u32[]{:S(2)}) copy-start(bf16[2,4,96,768]{3,2,1,0:T(8,128)(2,1)S(1)} %collective-permute-done.2.refs_4_) | copy-start | bytes 3538948
  204.3 1.0 copy-start.1

commit v3 on v2

--- a/solution.py
+++ b/solution.py
@@ -377,10 +377,11 @@
 
 
 def opening_kernel(n_z, count, *refs):
-    x_ref, gain_ref, bias_ref, sel_ref, table_ref, qkv_ref, proj_ref, up_ref, down_ref = refs[:9]
-    n_out, mod_out, w_outs = refs[9], refs[10], refs[11 : 11 + count]
-    w_refs = refs[11 + count : 11 + 2 * count]
-    n_ref, mod_s, local_sem, send_sem, recv_sem = refs[11 + 2 * count :]
+    x_ref, gain_ref, bias_ref, sel_ref, embed_ref, time_ref, time_bias_ref = refs[:7]
+    qkv_ref, proj_ref, up_ref, down_ref = refs[7:11]
+    n_out, mod_out, w_outs = refs[11], refs[12], refs[13 : 13 + count]
+    w_refs = refs[13 + count : 13 + 2 * count]
+    n_ref, mod_s, table_ref, local_sem, send_sem, recv_sem = refs[13 + 2 * count :]
     links = Links(send_sem, recv_sem, n_z)
     head_width = qkv_ref.shape[2]
     for part in range(3):
@@ -396,13 +397,74 @@
     def n_at(rank):
         return n_out.at[pl.ds(pl.multiple_of(rank * rows, rows), rows)]
 
+    z, x = links.z, links.x
+    right = {"dp": 2 * ((z + 1) % n_z) + x}
+    left = {"dp": 2 * ((z + n_z - 1) % n_z) + x}
+    right_slots = [links.slots(n_z) for _ in range(count)]
+    left_slots = [links.slots(n_z) for _ in range(count)]
+    side_slots = [links.slots(n_z) for _ in range(count)]
+    cross_slots = links.slots(2 * n_z)
+
     def w_at(n, rank):
         return w_outs[n].at[0, rank] if n in (1, 2) else w_outs[n].at[rank]
 
-    crossed = []
-
-    def cross(rank):
-        crossed.append(links.send(w_outs[2].at[0, rank], w_outs[2].at[1, rank], links.across))
+    def own_or(n, j, src):
+        return w_at(n, 2 * j + x) if src is None else src
+
+    def right_copy(n, j, src=None):
+        here = w_at(n, 2 * j + x)
+        return links.copy(own_or(n, j, src), here, right, right_slots[n] + j)
+
+    def left_copy(n, j, src=None):
+        here = w_at(n, 2 * j + x)
+        return links.copy(own_or(n, j, src), here, left, left_slots[n] + j)
+
+    def side_copy(n, j, src=None):
+        here = w_at(n, 2 * j + x)
+        return links.copy(own_or(n, j, src), here, links.beside, side_slots[n] + j)
+
+    def cross_copy(rank):
+        return links.copy(
+            w_outs[2].at[0, rank], w_outs[2].at[1, rank], links.across, cross_slots + rank
+        )
+
+    def arrived(n, j):
+        side_copy(n, j).start()
+        if n == 2:
+            cross_copy(2 * j + x).start()
+
+    def travel(n):
+        def step(d, carry):
+            @pl.when(z - d >= 0)
+            def _():
+                right_copy(n, z - d).wait_recv()
+
+                @pl.when(z < n_z - 1)
+                def _():
+                    right_copy(n, z - d).start()
+
+                arrived(n, z - d)
+
+            @pl.when(z + d <= n_z - 1)
+            def _():
+                left_copy(n, z + d).wait_recv()
+
+                @pl.when(z > 0)
+                def _():
+                    left_copy(n, z + d).start()
+
+                arrived(n, z + d)
+
+            return carry
+
+        lax.fori_loop(1, n_z, step, 0)
+
+    def each(body):
+        def step(j, carry):
+            body(j)
+            return carry
+
+        lax.fori_loop(0, n_z, step, 0)
 
     def norm_step(i, carry):
         here = pl.ds(pl.multiple_of(i * ROWS, ROWS), ROWS)
@@ -423,10 +485,17 @@
         copy.start()
         return copy
 
-    near, far = [], []
     for n in range(count):
-        near.append([links.send(w_refs[n], w_at(n, links.dp), links.along(k)) for k in range(1, n_z)])
-        far.append([links.send(w_refs[n], w_at(n, links.dp), links.beside)])
+
+        @pl.when(z < n_z - 1)
+        def _():
+            right_copy(n, z, w_refs[n]).start()
+
+        @pl.when(z > 0)
+        def _():
+            left_copy(n, z, w_refs[n]).start()
+
+        side_copy(n, z, w_refs[n]).start()
     lax.fori_loop(0, rows // ROWS, norm_step, 0)
     tiles = rows // ROWS
     mod_copies = []
@@ -437,31 +506,38 @@
         copy.start()
     n_y = links.send(n_ref, n_at(links.t), links.across)
     n_core = links.send(n_ref, n_at(links.t), links.core)
+    table_ref[...] = (
+        lax.dot_general(
+            embed_ref[...],
+            time_ref[...],
+            (((1,), (0,)), ((), ())),
+            precision=highest,
+            preferred_element_type=F32,
+        )
+        + time_bias_ref[...][None, :]
+    )
     others = []
     for n in range(count):
-        for k in range(1, n_z):
-            near[n][k - 1].wait_recv()
-            rank = 2 * ((links.z + n_z - k) % n_z) + links.x
-            far[n].append(links.send(w_at(n, rank), w_at(n, rank), links.beside))
-            if n == 2:
-                cross(rank)
+        travel(n)
         if n < 2:
             for i in range(n * tiles // 2, (n + 1) * tiles // 2):
                 mod_copies.append(mod_step(i))
         if n == 2:
             local[1 + n].wait()
-            cross(links.dp)
+            cross_copy(links.dp).start()
         if n == 1:
             n_y.wait_recv()
             n_relay = links.send(n_at(links.y_rank), n_at(links.y_rank), links.core)
-            for copy in far[n]:
-                copy.wait_recv()
+            each(lambda j: side_copy(1, j).wait_recv())
             local[1 + n].wait()
             others.append(links.send(w_outs[n].at[0], w_outs[n].at[2], links.across))
             others.append(links.send(w_outs[n].at[0], w_outs[n].at[1], links.core))
-    for k in range(n_z):
-        far[2][k].wait_recv()
-        cross(2 * ((links.z + n_z - k) % n_z) + 1 - links.x)
+
+    def late_cross(j):
+        side_copy(2, j).wait_recv()
+        cross_copy(2 * j + 1 - x).start()
+
+    each(late_cross)
     others[0].wait_recv()
     others.append(links.send(w_outs[1].at[2], w_outs[1].at[3], links.core))
     n_core.wait_recv()
@@ -470,20 +546,35 @@
     others[2].wait_recv()
     for n in range(count):
         if n not in (1, 2):
-            for copy in far[n]:
-                copy.wait_recv()
+            each(lambda j: side_copy(n, j).wait_recv())
             local[1 + n].wait()
-        for copy in near[n] + far[n]:
-            copy.wait_send()
-    for copy in crossed:
-        copy.wait_recv()
-    for copy in [n_y, n_core, n_relay] + others + crossed:
+
+        def drain(j):
+            side_copy(n, j).wait_send()
+
+            @pl.when((j <= z) & (z < n_z - 1))
+            def _():
+                right_copy(n, j).wait_send()
+
+            @pl.when((j >= z) & (z > 0))
+            def _():
+                left_copy(n, j).wait_send()
+
+        each(drain)
+
+    def crossed(j):
+        for rank in (2 * j, 2 * j + 1):
+            cross_copy(rank).wait_recv()
+            cross_copy(rank).wait_send()
+
+    each(crossed)
+    for copy in [n_y, n_core, n_relay] + others:
         copy.wait_send()
     for copy in local[:1] + mod_copies:
         copy.wait()
 
 
-def opening(x, gain, bias, sel, table, weights, n_dp, n_tensor):
+def opening(x, gain, bias, sel, embed, time_weight, time_bias, weights, n_dp, n_tensor):
     rows, width = x.shape
     n_z = n_dp // 2
     qkv, proj, up, down = weights
@@ -491,24 +582,25 @@
     early = up.shape[1] * 2 // 3 // 128 * 128
     columns = (3 * qkv.shape[2], proj.shape[0], early, down.shape[1], up.shape[1] - early)
     count = len(columns)
-    slots = count * (2 * n_z - 1) + 6 + n_dp
+    slots = 3 * count * n_z + 6 + n_dp
     shapes = [(n_dp, depth, c) for c in columns]
     shapes[1] = (n_tensor,) + shapes[1]
     shapes[2] = (2,) + shapes[2]
     return pl.pallas_call(
         functools.partial(opening_kernel, n_z, count),
         name="opening",
-        in_specs=[pl.BlockSpec(memory_space=pltpu.VMEM)] * 9,
+        in_specs=[pl.BlockSpec(memory_space=pltpu.VMEM)] * 11,
         out_specs=[pl.BlockSpec(memory_space=pl.ANY)] * (2 + count),
         out_shape=[
             jax.ShapeDtypeStruct((n_tensor * rows, width), BF),
-            jax.ShapeDtypeStruct((rows, table.shape[1]), F32),
+            jax.ShapeDtypeStruct((rows, time_weight.shape[1]), F32),
         ]
         + [jax.ShapeDtypeStruct(shape, BF) for shape in shapes],
         scratch_shapes=[pltpu.VMEM((depth, c), BF) for c in columns]
         + [
             pltpu.VMEM((rows, width), BF),
-            pltpu.VMEM((rows, table.shape[1]), F32),
+            pltpu.VMEM((rows, time_weight.shape[1]), F32),
+            pltpu.VMEM((embed.shape[0], time_weight.shape[1]), F32),
             pltpu.SemaphoreType.DMA((1 + count + rows // ROWS,)),
             pltpu.SemaphoreType.DMA((slots,)),
             pltpu.SemaphoreType.DMA((slots,)),
@@ -517,7 +609,7 @@
             collective_id=0, has_side_effects=True, vmem_limit_bytes=VMEM_LIMIT
         ),
         cost_estimate=pl.CostEstimate(flops=0, bytes_accessed=64 << 20, transcendentals=0),
-    )(x, gain, bias, sel, table, *weights)
+    )(x, gain, bias, sel, embed, time_weight, time_bias, *weights)
 
 
 def closing_kernel(n_z, slot_count, embed_width, *refs):
@@ -527,15 +619,15 @@
     up_out, down_out, proj_out, qkv_out = refs[18:22]
     all_ref, part_send, core_buf, y_send, y_recv, vec, all_vec, qkv_flat, qkv_ref = refs[22:31]
     up_y_send, up_y_recv = refs[31:33]
-    x_send, x_recv = refs[33:35], refs[35:38]
-    z_send, z_recv = refs[38:42], refs[42:46]
-    send_sem, recv_sem = refs[46:]
+    x_send, x_recv = refs[33], refs[34:37]
+    proj_y_send, proj_y_recv = refs[37:39]
+    z_send, z_recv = refs[39:43], refs[43:47]
+    send_sem, recv_sem = refs[47:]
     links = Links(send_sem, recv_sem, n_z)
     z, x = links.z, links.x
     n_dp = 2 * n_z
     rows, width = x_ref.shape
     outs = (up_out, down_out, proj_out, qkv_out)
-    pairs = (None, (down_near, down_far), (proj_near, proj_far))
     dp_peers = [{"dp": (links.dp + k) % n_dp} for k in range(1, n_dp)]
     diagonal = {"tensor": 3 - links.t}
     ranks = [links.t, links.core_rank, links.y_rank, 3 - links.t]
@@ -550,6 +642,7 @@
     all_ref[:, :, own_lanes] = sums_ref[...]
     up_slots = links.slots(n_z)
     x_slots = [None] + [links.slots(n_z) for _ in range(3)]
+    proj_slots = links.slots(2 * n_z)
     z_slots = [links.slots(n_z) for _ in range(4)]
     order = list(range(1, n_z)) + [0]
 
@@ -560,30 +653,54 @@
         return links.copy(up_y_send.at[s], up_y_recv.at[s], links.across, up_slots + s)
 
     def x_copy(n, s):
-        src = qkv_ref.at[at(s), 1 - x] if n == 3 else x_send[n - 1].at[s]
+        src = qkv_ref.at[at(s), 1 - x] if n == 3 else x_send.at[s]
         return links.copy(src, x_recv[n - 1].at[s], links.beside, x_slots[n] + s)
 
     def z_copy(n, s):
         peer = {"dp": 2 * at(s) + x}
         return links.copy(z_send[n].at[s], z_recv[n].at[s], peer, z_slots[n] + s)
 
-    def both(n, s, side):
-        near, far = pairs[n]
-        return near[at(s), side].astype(F32) + far[at(s), side].astype(F32)
+    def proj_copy(e, s):
+        src = (proj_near, proj_far)[e].at[at(s), 1 - x]
+        slot = (x_slots[2], proj_slots)[e] + s
+        return links.copy(src, x_recv[1].at[e, s], links.beside, slot)
+
+    def proj_y_copy(s):
+        slot = proj_slots + n_z + s
+        return links.copy(proj_y_send.at[s], proj_y_recv.at[s], links.across, slot)
+
+    def both(s, side):
+        return down_near[at(s), side].astype(F32) + down_far[at(s), side].astype(F32)
 
     def x_start(n):
         for s in order:
-            if n < 3:
-                x_send[n - 1][s] = both(n, s, 1 - x).astype(BF)
+            if n == 2:
+                proj_copy(1, s).start()
+                proj_copy(0, s).start()
+                continue
+            if n == 1:
+                x_send[s] = both(s, 1 - x).astype(BF)
             x_copy(n, s).start()
+
+    def proj_cross():
+        for s in order:
+            proj_copy(1, s).wait_recv()
+            own = proj_far[at(s), x].astype(F32) + x_recv[1][1, s].astype(F32)
+            proj_y_send[s] = own.astype(BF)
+            proj_y_copy(s).start()
 
     def value(n, s):
         if n == 0:
             up_copy(s).wait_recv()
             own = up_keep[0, at(s)].astype(F32) + up_got[0, at(s)].astype(F32)
             return own + up_y_recv[s].astype(F32)
+        if n == 2:
+            proj_copy(0, s).wait_recv()
+            proj_y_copy(s).wait_recv()
+            own = proj_near[at(s), x].astype(F32) + x_recv[1][0, s].astype(F32)
+            return own + proj_y_recv[s].astype(F32)
         x_copy(n, s).wait_recv()
-        own = qkv_ref[at(s), x].astype(F32) if n == 3 else both(n, s, x)
+        own = qkv_ref[at(s), x].astype(F32) if n == 3 else both(s, x)
         return own + x_recv[n - 1][s].astype(F32)
 
     def z_start(n):
@@ -607,14 +724,12 @@
         up_copy(s).start()
     x_start(2)
     part_send[0] = part(3).astype(BF)
-    part_send[1] = part(1).astype(BF)
     c3 = links.send(part_send.at[0], core_buf.at[0], links.core)
-    z_start(1)
-    c1 = links.send(part_send.at[1], core_buf.at[1], links.core)
     far = part(2)
     c3.wait_recv()
     y_send[...] = (far + core_buf[0].astype(F32)).astype(BF)
-
+    part_send[1] = part(1).astype(BF)
+    y_copy = links.send(y_send, y_recv, links.across)
     strip = 256
 
     def qkv_step(j, carry):
@@ -622,13 +737,15 @@
         qkv_flat[here, :] = dot(g_ref[...], n_ref[:, here], 1, 0).T.astype(BF)
         return carry
 
-    y_copy = links.send(y_send, y_recv, links.across)
+    c1 = links.send(part_send.at[1], core_buf.at[1], links.core)
+    z_start(1)
     lax.fori_loop(0, width // strip, qkv_step, 0)
     depth = qkv_ref.shape[2]
     for r in range(n_dp):
         qkv_ref[r // 2, r % 2] = qkv_flat[r * depth : (r + 1) * depth, :]
+    x_start(3)
+    proj_cross()
     z_start(0)
-    x_start(3)
     z_start(2)
     near = part(0)
     c1.wait_recv()
@@ -687,8 +804,11 @@
         copy.wait_send()
     for s in range(n_z):
         up_copy(s).wait_send()
+        proj_copy(0, s).wait_send()
+        proj_copy(1, s).wait_send()
+        proj_y_copy(s).wait_send()
         for n in range(4):
-            if n > 0:
+            if n in (1, 3):
                 x_copy(n, s).wait_send()
             if s > 0:
                 z_copy(n, s).wait_send()
@@ -708,7 +828,7 @@
     columns = [up[0].shape[-1], down[0].shape[-1], proj[0].shape[-1], head_width]
     shards = [(depth, c) for c in columns]
     stacks = [(n_z,) + shard for shard in shards]
-    slots = 8 * n_z + 2 + 1 + 3 + 3 + (n_dp - 1)
+    slots = 10 * n_z + 2 + 1 + 3 + 3 + (n_dp - 1)
     vmem = pl.BlockSpec(memory_space=pltpu.VMEM)
     out = pl.pallas_call(
         functools.partial(closing_kernel, n_z, slot_count, embed_width),
@@ -736,8 +856,8 @@
             pltpu.VMEM(stacks[0], BF),
             pltpu.VMEM(stacks[0], BF),
         ]
-        + [pltpu.VMEM(shape, BF) for shape in stacks[1:3]]
-        + [pltpu.VMEM(shape, BF) for shape in stacks[1:]]
+        + [pltpu.VMEM(shape, BF) for shape in (stacks[1], stacks[1], (2,) + stacks[2], stacks[3])]
+        + [pltpu.VMEM(shape, BF) for shape in (stacks[2], stacks[2])]
         + [pltpu.VMEM(shape, BF) for _ in range(2) for shape in stacks]
         + [pltpu.SemaphoreType.DMA((slots,)), pltpu.SemaphoreType.DMA((slots,))],
         compiler_params=pltpu.CompilerParams(
@@ -1216,7 +1336,6 @@
     slots = jnp.arange(slot_count, dtype=jnp.int32)
     onehot = (own_segment[:, None] == slots[None, :]).astype(F32)
     embedded = time_embed(timesteps[0], time_weight.shape[0])
-    mod_table = jnp.dot(embedded, time_weight, precision=highest) + time_bias
     sums_rows = -(-(slot_count + 1 + n_tensor) // 8) * 8
     chosen = (own_segment[None, :] == jnp.arange(sums_rows, dtype=jnp.int32)[:, None]) & (
         own_segment[None, :] < slot_count
@@ -1230,7 +1349,9 @@
         norm_gain,
         norm_bias,
         onehot,
-        mod_table,
+        embedded,
+        time_weight,
+        time_bias,
         (qkv_weight, proj_weight, up_weight, down_weight.T),
         n_dp,
         n_tensor,
@@ -1271,7 +1392,6 @@
         queries, keys, values, mixed_grad, mixed, log_totals, seg_row, seg_col, cos, sin, lo, hi
     )
 
-    proj_far = to_tensor_peer(proj_other, 2)
     down_far = to_tensor_peer(down_other, 2)
     up_got = lax.ppermute(up_away, "dp", [(r, r ^ 1) for r in range(n_dp)])
 
@@ -1281,7 +1401,7 @@
         qkv_full,
         (up_keep, up_got),
         (down_near, down_far),
-        (proj_near, proj_far),
+        (proj_near, proj_other),
         residual_in,
         hidden_grad,
         norm_gain,

time: 277 us -> 265 us (0.957)
  waiting for transfers between devices: 8.03 us -> 2.01 us
  Pallas kernels: 247 us -> 243 us
    ppermute x4 -> x3, waiting for transfers between devices: 8.03 us -> 2.01 us  [to_tensor_peer(): lax.ppermute(value, 'tensor', [(r, r ^ distance) for r in range(size)])]
    pallas_call x1, Pallas kernels: 66.9 us -> 63.9 us  [middle(): pl.pallas_call(functools.partial(middle_kernel, n_dp // 2), name='middle'...]
  transfers between devices with their start and end apart: 5 -> 4, of which waited for: 2 -> 2; matrix products, arithmetic and copies ran while one was open for 2% -> 2% of each run, Pallas kernels for 18% -> 19%
where the time goes in v3:
time: 265 us; the launch traced here: 263 us
  Pallas kernels  243 us (92%)
  other arithmetic  7.12 us (3%)
  starting transfers between devices  6.73 us (3%)
  local copies, waits for them, and re-layouts  3.22 us (1%)
    pallas_call x1, Pallas kernels, middle(): pl.pallas_call(functools.partial(middle_kernel, n_dp // 2), name='middle'...  63.9 us
    pallas_call x1, Pallas kernels, closing(): pl.pallas_call(functools.partial(closing_kernel, n_z, slot_count, embed_w...  63.6 us
    pallas_call x1, Pallas kernels, opening(): pl.pallas_call(functools.partial(opening_kernel, n_z, count), name='openi...  60.4 us
    pallas_call x1, Pallas kernels, attend_back(): pl.pallas_call(functools.partial(attend_back_kernel, heads), name='attend...  26.4 us
    pallas_call x1, Pallas kernels, attend(): pl.pallas_call(functools.partial(attend_kernel, heads), name='attend', gr...  18 us
    pallas_call x1, Pallas kernels, project(): pl.pallas_call(functools.partial(project_kernel, heads), name='project_qk...  5.95 us
  transfers between devices with their start and end apart: 4, of which 2 were waited for; matrix products, arithmetic and copies ran while one was open for 2% of the time, Pallas kernels for 19%

profile of v3, /device:TPU:0, one launch (start us, length us, event | category | flops | bytes accessed | tf_op | source)
XLA Modules:
  0.0 263.3 jit_solution(2742618553399140241)
XLA Ops:
  0.7 0.7 convert_bitcast_fusion
  1.3 0.7 copy.32
  2.1 0.1 reduce
  2.2 0.8 select_reduce_fusion
  3.0 0.1 broadcast_compare_fusion
  3.1 0.8 fusion.refs_3_
  3.9 0.1 multiply_cosine_fusion.1
  4.0 0.7 broadcast_select_fusion
  4.7 60.4 %opening.1 = (bf16[2048,768]{1,0:T(8,128)(2,1)}, f32[512,2304]{1,0:T(8,128)}, bf16[8,96,576]{2,1,0:T(8,128)(2,1)}, bf16[4,8,96,192]{3,2,1,0:T(8,128)(2,1)}, bf16...) custom-call(f32[512,768]{1,0:T(8,128)} %refs_9_.3, f32[768]{0:T(1024)} %refs_11_.1, ...), custom_call_target="tpu_custom_call" | custom-call | bytes 67108864 | tf_op jit(solution)/shard_map/opening/pallas_call | solution.py:589
  65.2 0.6 collective-permute-start
  65.7 1.5 collective-permute-start.1
  67.3 1.3 copy.33.scol_ref
  68.6 0.2 select_reduce_fusion.1
  68.9 0.5 and_select_fusion
  69.4 1.8 multiply_sine_fusion
  71.2 6.0 %project_qkv.1 = (bf16[192,2048]{1,0:T(8,128)(2,1)}, bf16[192,2048]{1,0:T(8,128)(2,1)}, bf16[192,2048]{1,0:T(8,128)(2,1)}) custom-call(bf16[2048,768]{1,0:T(8,128)(2,1)} %get-tuple-element.57.n_ref.refs_1_, bf16[768,576]{1,0:T(8,128)(2,1)} %bitcast.19, f32[32,2048]{1,0:T(8,128)} %get-tuple-element.114.cos_ref, f32[32,2048]{1,0:T(8,128)} %get-tuple-element.113.sin_ref), custom_call_target="tpu_custom_call" | custom-call | flops 1811939328 | bytes 8388608 | tf_op jit(solution)/shard_map/project_qkv/pallas_call | solution.py:103
  77.1 18.0 %attend.1 = (bf16[192,2048]{1,0:T(8,128)(2,1)}, f32[3,2048]{1,0:T(4,128)}) custom-call(s32[4]{0:T(128)} %get-tuple-element.118.lo_ref, s32[4]{0:T(128)} %get-tuple-element.117.hi_ref, bf16[192,2048]{1,0:T(8,128)(2,1)} %get-tuple-element.59.q_ref, bf16[192,2048]{1,0:T(8,128)(2,1)} %get-tuple-element.60.k_ref, bf16[192,2048]{1,0:T(8,128)(2,1)} %get-tuple-element.61.v_ref, ...), custom_call_target="tpu_custom_call" | custom-call | flops 6442450944 | bytes 8388608 | tf_op jit(solution)/shard_map/attend/pallas_call | solution.py:174
  95.2 0.1 fusion.3
  95.3 0.6 pad_maximum_fusion.refs_13_
  95.9 0.6 fusion.2.refs_10_
  96.5 0.0 collective-permute-done.refs_4_
  96.6 1.4 collective-permute-done.1.refs_6_
  98.0 63.9 %middle.1 = (f32[512,768]{1,0:T(8,128)}, f32[512,768]{1,0:T(8,128)}, bf16[192,2048]{1,0:T(8,128)(2,1)}, f32[8,24,640]{2,1,0:T(8,128)}, bf16[768,768]{1,0:T(8,128...) custom-call(bf16[192,2048]{1,0:T(8,128)(2,1)} %get-tuple-element.62., ...), custom_call_target="tpu_custom_call" | custom-call | flops 14495514624 | bytes 67108864 | tf_op jit(solution)/shard_map/middle/pallas_call | solution.py:1177
  161.9 3.1 %collective-permute-start.2 = (bf16[2,4,96,768]{3,2,1,0:T(8,128)(2,1)}, bf16[2,4,96,768]{3,2,1,0:T(8,128)(2,1)S(1)}, u32[]{:S(2)}, u32[]{:S(2)}) collective-permute-start(bf16[2,4,96,768]{3,2,1,0:T(8,128)(2,1)} %get-tuple-element.72), channel_id=1, source_target_pairs={{0,4},{4,0},{8,12},{12,8},{16,20},{20,16},{24,28},{28,24},{1,5},{5... | collective-permute-start | bytes 3538952 | tf_op jit(solution)/shard_map/ppermute | solution.py:1396
  165.0 1.5 collective-permute-start.3
  166.5 26.4 %attend_back.1.refs_0_ = bf16[576,2048]{1,0:T(8,128)(2,1)} custom-call(s32[4]{0:T(128)} %get-tuple-element.118.lo_ref, s32[4]{0:T(128)} %get-tuple-element.117.hi_ref, bf16[192,2048]{1,0:T(8,128)(2,1)} %get-tuple-element.59.q_ref, bf16[192,2048]{1,0:T(8,128)(2,1)} %get-tuple-element.60.k_ref, bf16[192,2048]{1,0:T(8,128)(2,1)} %get-tuple-element.61.v_ref, ...), custom_call_target="tpu_custom_call" | custom-call | flops 16106127360 | bytes 8388608 | tf_op jit(solution)/shard_map/attend_back/pallas_call | solution.py:298
  192.9 0.0 collective-permute-done.2.refs_4_
  192.9 0.6 collective-permute-done.3
  193.5 0.4 copy-done
  193.9 0.6 copy-done.1
  194.5 63.6 %closing.1 = (f32[512,768]{1,0:T(8,128)}, f32[1,1536]{1,0:T(1,128)}, f32[128,2304]{1,0:T(8,128)}, f32[1,2304]{1,0:T(1,128)}, f32[8,1536]{1,0:T(8,128)}, /*index=...) custom-call(bf16[576,2048]{1,0:T(8,128)(2,1)} %attend_back.1.refs_0_, ...), custom_call_target="tpu_custom_call" | custom-call | bytes 67108864 | tf_op jit(solution)/shard_map/closing/pallas_call | solution.py:833
  258.1 5.0 %results.1 = (f32[512,768]{1,0:T(8,128)}, f32[512,768]{1,0:T(8,128)}, f32[768]{0:T(1024)}, f32[768]{0:T(1024)}, f32[3,96,192]{2,1,0:T(8,128)}, /*index=5*/f32[19...) custom-call(f32[512,768]{1,0:T(8,128)} %get-tuple-element.68.refs_0_, ...), custom_call_target="tpu_custom_call" | custom-call | tf_op jit(solution)/shard_map/results/pallas_call | solution.py:1290
  (20 shorter events, 0.1 us)
Async XLA Ops:
  3.0 64.3 %copy-start.2 = (s32[2048]{0:T(1024)}, s32[2048]{0:T(1024)S(1)}, u32[]{:S(2)}) copy-start(s32[2048]{0:T(1024)S(1)} %get-tuple-element.102) | copy-start | bytes 24580
  4.7 63.9 %copy-start.4 = (s32[1,16]{1,0:T(1,128)S(1)}, s32[1,16]{1,0:T(1,128)}, u32[]{:S(2)}) copy-start(s32[1,16]{1,0:T(1,128)} %param.17) | copy-start | bytes 196
  65.2 31.4 %collective-permute-start = (bf16[768,256]{1,0:T(8,128)(2,1)}, bf16[768,256]{1,0:T(8,128)(2,1)S(1)}, u32[]{:S(2)}, u32[]{:S(2)}) collective-permute-start(bf16[768,256]{1,0:T(8,128)(2,1)} %bitcast.34), channel_id=1, source_target_pairs={{0,2},{1,3},{2,0},{3,1},{4,6},{5,7},{6,4},{7,5},{8,10},{9,11},{10,... | collective-permute-start | bytes 1179656 | tf_op jit(solution)/shard_map/ppermute | solution.py:1302
  65.7 32.3 %collective-permute-start.1 = (bf16[768,768]{1,0:T(8,128)(2,1)}, bf16[768,768]{1,0:T(8,128)(2,1)}, u32[]{:S(2)}, u32[]{:S(2)}) collective-permute-start(bf16[768,768]{1,0:T(8,128)(2,1)} %bitcast.32), channel_id=1, source_target_pairs={{0,2},{1,3},{2,0},{3,1},{4,6},{5,7},{6,4},{7,5},{8,10},{9,11},{10,... | collective-permute-start | bytes 3538952 | tf_op jit(solution)/shard_map/ppermute | solution.py:1302
  77.1 18.0 %copy-start.3 = (f32[3072]{0:T(1024)S(1)}, f32[3072]{0:T(1024)}, u32[]{:S(2)}) copy-start(f32[3072]{0:T(1024)} %param.25) | copy-start | bytes 36868
  96.6 1.4 copy-start.5
  161.9 31.0 %collective-permute-start.2 = (bf16[2,4,96,768]{3,2,1,0:T(8,128)(2,1)}, bf16[2,4,96,768]{3,2,1,0:T(8,128)(2,1)S(1)}, u32[]{:S(2)}, u32[]{:S(2)}) collective-permute-start(bf16[2,4,96,768]{3,2,1,0:T(8,128)(2,1)} %get-tuple-element.72), channel_id=1, source_target_pairs={{0,4},{4,0},{8,12},{12,8},{16,20},{20,16},{24,28},{28,24},{1,5},{5... | collective-permute-start | bytes 3538952 | tf_op jit(solution)/shard_map/ppermute | solution.py:1396
  165.0 28.5 %collective-permute-start.3 = (bf16[768,768]{1,0:T(8,128)(2,1)}, bf16[768,768]{1,0:T(8,128)(2,1)S(1)}, u32[]{:S(2)}, u32[]{:S(2)}) collective-permute-start(bf16[768,768]{1,0:T(8,128)(2,1)} %get-tuple-element.74), channel_id=1, source_target_pairs={{0,2},{1,3},{2,0},{3,1},{4,6},{5,7},{6,4},{7,5},{8,10},{9,11},{10,... | collective-permute-start | bytes 3538952 | tf_op jit(solution)/shard_map/ppermute | solution.py:1302
  192.9 1.0 copy-start
  193.5 1.0 copy-start.1
